TPU v7x, 128 devices: a whole 4x4x4 slice. The times are simulated.
128 devices in a mesh: gx: 2 (over core), gy: 4 (over x), gz: 16 (over z, y).
Axes of the slice: x: 4, y: 4, z: 4, core: 2. Of those that a mesh axis runs over, the one named last changes fastest.
Arguments:
- right_side: float32 [96, 192, 768], P('gx', 'gy', 'gz'), may hold values from -6 to 6
- start_guess: float32 [96, 192, 768], P('gx', 'gy', 'gz'), may hold values from -3 to 3
- reaction: float32 [96, 192, 768], P('gx', 'gy', 'gz'), may hold values from 0.0005 to 0.005
Outputs:
- solution_field: float32 [96, 192, 768], P('gx', 'gy', 'gz')
- residual: float32 [96, 192, 768], P('gx', 'gy', 'gz')
All inputs are finite; a program needn't handle non-finite values.
Results may differ from a plain program's by a relative error of at most 0.0003.
Values sent between devices are 32-bit elements.
A program may use at most 128 MiB of HBM per device.

v0:
```python
import jax
import jax.numpy as jnp
from jax import lax
from jax.experimental import pallas as pl
from jax.experimental.pallas import tpu as pltpu
from jax.sharding import PartitionSpec as P

LEVELS = 5
BOTTOM_ITERS = 6
LOCAL = 2
AXES = ("gx", "gy", "gz")
MESH = pl.DeviceIdType.MESH
F32 = jnp.float32

damping = 6.0 / 7.0


def up_to(n, m):
    return -(-n // m) * m


def lanes_of(shape):
    return up_to(max(shape[2] + 1, shape[0]), 128)


def halved(shape, times):
    return tuple(s >> times for s in shape)


def loop(n, f, carry=0, unroll=4):
    while n % unroll:
        unroll -= 1

    def step(i, c):
        for k in range(unroll):
            c = f(i * unroll + k, c)
        return c

    return lax.fori_loop(0, n // unroll, step, carry)


def lane_of(rows, lanes):
    return lax.broadcasted_iota(jnp.int32, (rows, lanes), 1)


def pick(lanes_in, lanes_out, f, value):
    r = lax.broadcasted_iota(jnp.int32, (lanes_in, lanes_out), 0)
    c = lax.broadcasted_iota(jnp.int32, (lanes_in, lanes_out), 1)
    return jnp.where(f(r, c), value, 0.0).astype(F32)


def dot(a, b):
    return lax.dot(a, b, precision=lax.Precision.HIGHEST, preferred_element_type=F32)


def total(v):
    v = jnp.sum(v, axis=0, keepdims=True)
    return jnp.sum(v, axis=1, keepdims=True)


def fold(v):
    out = v[0:8]
    for k in range(1, v.shape[0] // 8):
        out = out + v[8 * k : 8 * k + 8]
    return out


def make_kernel(sizes, block):
    nx, ny, nz = sizes
    whole = (block[0] * nx, block[1] * ny, block[2] * nz)
    shapes = [halved(block, k) if k < LOCAL else halved(whole, k) for k in range(LEVELS)]
    lanes = [lanes_of(s) for s in shapes]
    counts = [6, 4]
    part = halved(block, LOCAL)
    wide = shapes[LOCAL][2]
    packs = 2 if wide <= 64 and part[0] % 2 == 0 else 1
    slabs = part[0] // packs
    rows = up_to(part[1], 8)
    glanes = lanes[LOCAL]
    half = glanes // packs

    scratch = {}
    for k in range(LEVELS):
        X, Y, Z = shapes[k]
        L = lanes[k]
        Yp = up_to(Y, 8)
        n = counts[k] if k < LOCAL else 2
        scratch[f"e{k}"] = pltpu.VMEM((n, X + 2, Yp + 16, L), F32)
        scratch[f"f{k}"] = pltpu.VMEM((X, Yp, L), F32)
        scratch[f"s{k}"] = pltpu.VMEM((X, Yp, L), F32)
        scratch[f"w{k}"] = pltpu.VMEM((X, Yp, L), F32)
        if k < LEVELS - 1:
            scratch[f"t{k}"] = pltpu.VMEM((L // 128, X // 2, 2 * up_to(Y // 2, 8), 128), F32)
        if k < LOCAL:
            for name, n_rows in (("zs", Y), ("zr", Y), ("ys", X), ("yr", X)):
                scratch[f"{name}{k}"] = pltpu.VMEM((n, 2, n_rows, L), F32)
            scratch[f"send{k}"] = pltpu.SemaphoreType.DMA((n, 6))
            scratch[f"recv{k}"] = pltpu.SemaphoreType.DMA((n, 6))
    scratch["ap"] = pltpu.VMEM((block[0], block[1], lanes[0]), F32)
    for g in range(2):
        scratch[f"gz{g}"] = pltpu.VMEM((nz, slabs, rows, glanes), F32)
        scratch[f"gm{g}"] = pltpu.VMEM((slabs, rows, glanes), F32)
        scratch[f"gy{g}"] = pltpu.VMEM((slabs, ny * rows, glanes), F32)
        scratch[f"gx{g}"] = pltpu.VMEM((nx, slabs, ny * rows, glanes), F32)
    for i, n in enumerate(sizes):
        scratch[f"q{i}"] = pltpu.VMEM((n, 16, lanes[0]), F32)
        scratch[f"qs{i}"] = pltpu.VMEM((16, lanes[0]), F32)
    scratch["gsend"] = pltpu.SemaphoreType.DMA((3, 3, max(sizes)))
    scratch["grecv"] = pltpu.SemaphoreType.DMA((3, 3, max(sizes)))

    names = list(scratch)

    def kernel(rs_ref, sg_ref, re_ref, sol_ref, res_ref, *refs):
        R = dict(zip(names, refs))
        pos = [lax.axis_index(a) for a in AXES]

        def zero(ref):
            ref[...] = jnp.zeros(ref.shape, F32)

        for k in range(LEVELS):
            X, Y, Z = shapes[k]
            for b in range(R[f"e{k}"].shape[0]):
                zero(R[f"e{k}"].at[b, 0])
                zero(R[f"e{k}"].at[b, X + 1])
                if k >= LOCAL:
                    Yp = up_to(Y, 8)
                    for x in range(1, X + 1):
                        R[f"e{k}"][b, x, 0:8, :] = jnp.zeros((8, lanes[k]), F32)
                        R[f"e{k}"][b, x, Yp + 8 :, :] = jnp.zeros((8, lanes[k]), F32)
                else:
                    zero(R[f"zr{k}"].at[b, 0])
                    zero(R[f"zr{k}"].at[b, 1])
                    zero(R[f"yr{k}"].at[b, 0])
                    zero(R[f"yr{k}"].at[b, 1])
            if k < LEVELS - 1 and Y // 2 % 8:
                for m in range(lanes[k] // 128):
                    for x in range(X // 2):
                        R[f"t{k}"][m, x, Y:, :] = jnp.zeros((R[f"t{k}"].shape[2] - Y, 128), F32)

        barrier = pltpu.get_barrier_semaphore()
        for axis, n, me in zip(AXES, sizes, pos):
            for d in range(1, n):
                pl.semaphore_signal(barrier, inc=1, device_id={axis: lax.rem(me + d, n)}, device_id_type=MESH)
        pl.semaphore_wait(barrier, sum(n - 1 for n in sizes))

        pending = []

        def copies(k, b):
            X, Y, Z = shapes[k]
            e = R[f"e{k}"]
            zs, zr, ys, yr = (R[f"{m}{k}"] for m in ("zs", "zr", "ys", "yr"))
            out = []
            pairs = (
                (e.at[b, 1, pl.ds(8, Y), :], e.at[b, X + 1, pl.ds(8, Y), :]),
                (e.at[b, X, pl.ds(8, Y), :], e.at[b, 0, pl.ds(8, Y), :]),
                (ys.at[b, 0], yr.at[b, 1]),
                (ys.at[b, 1], yr.at[b, 0]),
                (zs.at[b, 0], zr.at[b, 1]),
                (zs.at[b, 1], zr.at[b, 0]),
            )
            for i, (src, dst) in enumerate(pairs):
                axis, me, n = AXES[i // 2], pos[i // 2], sizes[i // 2]
                target = me - 1 if i % 2 == 0 else me + 1
                low, high = me > 0, me < n - 1
                copy = pltpu.make_async_remote_copy(
                    src_ref=src,
                    dst_ref=dst,
                    send_sem=R[f"send{k}"].at[b, i],
                    recv_sem=R[f"recv{k}"].at[b, i],
                    device_id={axis: target},
                    device_id_type=MESH,
                )
                out.append((copy, low if i % 2 == 0 else high, high if i % 2 == 0 else low))
            return out

        def send(k, b):
            for copy, sends, _ in copies(k, b):
                pl.when(sends)(copy.start)
            pending.append((k, b))

        def receive(k, b):
            X, Y, Z = shapes[k]
            for copy, _, receives in copies(k, b):
                pl.when(receives)(copy.wait_recv)
            for x in range(X):
                R[f"e{k}"][b, x + 1, 7:8, :] = R[f"yr{k}"][b, 0, x : x + 1, :]
                R[f"e{k}"][b, x + 1, 8 + Y : 9 + Y, :] = R[f"yr{k}"][b, 1, x : x + 1, :]

        def applied(k, b, x, split):
            X, Y, Z = shapes[k]
            L = lanes[k]
            Yp = up_to(Y, 8)
            e = R[f"e{k}"]
            i = x + 1
            c = e[b, i, 8 : 8 + Yp, :]
            beside = e[b, i + 1, 8 : 8 + Yp, :] + e[b, i - 1, 8 : 8 + Yp, :]
            beside = beside + (e[b, i, 9 : 9 + Yp, :] + e[b, i, 7 : 7 + Yp, :])
            beside = beside + (pltpu.roll(c, 1, 1) + pltpu.roll(c, L - 1, 1))
            if split:
                lane = lane_of(Yp, L)
                low = pltpu.roll(R[f"zr{k}"][b, 0], lax.rem(L - x, L), 1)
                high = pltpu.roll(R[f"zr{k}"][b, 1], lax.rem(L + Z - 1 - x, L), 1)
                beside = beside + jnp.where(lane == 0, low, jnp.where(lane == Z - 1, high, 0.0))
            return c, 0.25**k * (6.0 * c - beside) + R[f"s{k}"][x] * c

        def produce(k, b, f):
            X, Y, Z = shapes[k]
            L = lanes[k]
            lane = lane_of(Y, L)

            def one(x, faces):
                low, high = faces
                v = f(x)
                R[f"e{k}"][b, x + 1, 8 : 8 + Y, :] = v
                R[f"ys{k}"][b, 0, pl.ds(x, 1), :] = v[0:1]
                R[f"ys{k}"][b, 1, pl.ds(x, 1), :] = v[Y - 1 : Y]
                low = jnp.where(lane == x, pltpu.roll(v, x, 1), low)
                high = jnp.where(lane == x, pltpu.roll(v, lax.rem(x + L - Z + 1, L), 1), high)
                return low, high

            low, high = loop(X, one, (jnp.zeros((Y, L), F32), jnp.zeros((Y, L), F32)))
            R[f"zs{k}"][b, 0] = low
            R[f"zs{k}"][b, 1] = high
            send(k, b)

        def relaxed(k, b, x, split):
            c, a = applied(k, b, x, split)
            return c + R[f"w{k}"][x] * (R[f"f{k}"][x] - a)

        def keep(k, j, n, v):
            for m in range(lanes[k] // 128):
                R[f"t{k}"][m, j, 0:n, :] = v[:, 128 * m : 128 * m + 128]

        def kept(k, j, n):
            v = [R[f"t{k}"][m, j, 0:n, :] for m in range(lanes[k] // 128)]
            return v[0] if len(v) == 1 else jnp.concatenate(v, axis=1)

        def double_rows(k, v):
            n = v.shape[1]
            for m in range(lanes[k] // 128):
                for d in range(2):
                    R[f"t{k}"][m, :, pl.ds(d, n, stride=2), :] = v[:, :, 128 * m : 128 * m + 128]

        def pairs_of(k, f):
            X, Y, Z = shapes[k]

            def one(j, c):
                keep(k, j, up_to(Y, 8), f(2 * j) + f(2 * j + 1))
                return c

            loop(X // 2, one, 0, 2)

        def halve_rows(k):
            t = R[f"t{k}"]
            n = t.shape[2] // 2
            v = [
                t[m, :, pl.ds(0, n, stride=2), :] + t[m, :, pl.ds(1, n, stride=2), :]
                for m in range(lanes[k] // 128)
            ]
            v = [u.reshape(u.shape[0] * n, 128) for u in v]
            return v[0] if len(v) == 1 else jnp.concatenate(v, axis=1)

        def coarsened(k):
            X, Y, Z = shapes[k]
            n = R[f"t{k}"].shape[2] // 2
            C = pick(lanes[k], lanes[k + 1], lambda r, c: (r // 2 == c) & (r < Z), 0.125)
            return dot(halve_rows(k), C).reshape(X // 2, n, lanes[k + 1])

        def weights(k):
            X, Y, Z = shapes[k]
            Yp = up_to(Y, 8)
            lane = lane_of(Yp, lanes[k])

            def one(x, c):
                s = jnp.where(lane < Z, R[f"s{k}"][x], 0.0)
                R[f"w{k}"][x] = jnp.where(lane < Z, damping / (6.0 * 0.25**k + s), 0.0)
                return c

            loop(X, one)

        def spread(g, stage):
            axis_at = 2 - stage
            axis, n, me = AXES[axis_at], sizes[axis_at], pos[axis_at]
            if stage == 0:
                src, dst = R[f"gz{g}"].at[me], R[f"gz{g}"].at[me]
            elif stage == 1:
                here = pl.ds(pl.multiple_of(me * rows, 8), rows)
                src, dst = R[f"gm{g}"], R[f"gy{g}"].at[:, here, :]
            else:
                src, dst = R[f"gy{g}"], R[f"gx{g}"].at[me]
            return [
                pltpu.make_async_remote_copy(
                    src_ref=src,
                    dst_ref=dst,
                    send_sem=R["gsend"].at[g, stage, d],
                    recv_sem=R["grecv"].at[g, stage, d],
                    device_id={axis: lax.rem(me + d, n)},
                    device_id_type=MESH,
                )
                for d in range(1, n)
            ]

        def gather_first(g):
            k = LOCAL - 1
            Z = shapes[k][2]
            v = halve_rows(k)
            v = v.reshape(packs, slabs * rows, v.shape[1])
            block_sum = None
            for h in range(packs):
                at = pos[2] * part[2] + h * half
                C = pick(lanes[k], glanes, lambda r, c: (r // 2 + at == c) & (r < Z), 0.125)
                piece = dot(v[h], C)
                block_sum = piece if block_sum is None else block_sum + piece
            R[f"gz{g}"][pos[2]] = block_sum.reshape(slabs, rows, glanes)
            for copy in spread(g, 0):
                copy.start()

        def gather_second(g):
            for copy in spread(g, 0):
                copy.wait_recv()
            v = R[f"gz{g}"][0]
            for i in range(1, nz):
                v = v + R[f"gz{g}"][i]
            R[f"gm{g}"][...] = v
            for copy in spread(g, 1):
                copy.start()
            R[f"gy{g}"][:, pl.ds(pl.multiple_of(pos[1] * rows, 8), rows), :] = v

        def gather_third(g):
            for copy in spread(g, 1):
                copy.wait_recv()
            for copy in spread(g, 2):
                copy.start()

        def gather_last(g, name):
            k = LOCAL
            lane = lane_of(part[1], glanes)
            R[f"gx{g}"][pos[0]] = R[f"gy{g}"][...]
            for copy in spread(g, 2):
                copy.wait_recv()
            for i in range(nx):
                for h in range(packs):
                    for j in range(slabs):
                        x = (i * packs + h) * slabs + j
                        for m in range(ny):
                            v = R[f"gx{g}"][i, j, m * rows : m * rows + part[1], :]
                            if h:
                                v = pltpu.roll(v, glanes - h * half, 1)
                            if packs > 1:
                                v = jnp.where(lane < wide, v, 0.0)
                            R[f"{name}{k}"][x, m * part[1] : (m + 1) * part[1], :] = v

        def gather_sends(g):
            for stage in range(3):
                for copy in spread(g, stage):
                    copy.wait_send()

        X, Y, Z = block
        L = lanes[0]

        def fill_guess(x):
            v = sg_ref[x]
            return jnp.concatenate([v, jnp.zeros((Y, L - Z), F32)], axis=1)

        produce(0, 0, fill_guess)

        def fill(x, c):
            v = jnp.concatenate([re_ref[x], jnp.zeros((Y, L - Z), F32)], axis=1)
            R["s0"][x] = v
            return c

        loop(X, fill)
        weights(0)
        for k in range(LOCAL):
            pairs_of(k, lambda x: R[f"s{k}"][x])
            if k < LOCAL - 1:
                R[f"s{k + 1}"][...] = coarsened(k)
                weights(k + 1)
            else:
                gather_first(0)

        receive(0, 0)

        def residual_of(x):
            c, a = applied(0, 0, x, True)
            f = jnp.concatenate([rs_ref[x], jnp.zeros((Y, L - Z), F32)], axis=1) - a
            R["f0"][x] = f
            return R["w0"][x] * f

        produce(0, 1, residual_of)
        gather_second(0)
        receive(0, 1)
        produce(0, 2, lambda x: relaxed(0, 1, x, True))
        gather_third(0)

        def left(k, b, x, split):
            c, a = applied(k, b, x, split)
            return R[f"f{k}"][x] - a

        receive(0, 2)
        pairs_of(0, lambda x: left(0, 2, x, True))
        R["f1"][...] = coarsened(0)
        produce(1, 0, lambda x: R["w1"][x] * R["f1"][x])
        gather_last(0, "s")
        for k in range(LOCAL, LEVELS):
            weights(k)
            if k < LEVELS - 1:
                pairs_of(k, lambda x: R[f"s{k}"][x])
                R[f"s{k + 1}"][...] = coarsened(k)
        receive(1, 0)
        produce(1, 1, lambda x: relaxed(1, 0, x, True))
        receive(1, 1)
        pairs_of(1, lambda x: left(1, 1, x, True))
        gather_first(1)
        gather_second(1)
        gather_third(1)
        gather_last(1, "f")

        def solve(k):
            X, Y, Z = shapes[k]
            Yp, L = up_to(Y, 8), lanes[k]
            e, f, w = R[f"e{k}"], R[f"f{k}"], R[f"w{k}"]

            def put(b, g):
                def one(x, c):
                    e[b, x + 1, 8 : 8 + Yp, :] = g(x)
                    return c

                loop(X, one)

            if k == LEVELS - 1:
                inside = (lane_of(Yp, L) < Z) & (lax.broadcasted_iota(jnp.int32, (Yp, L), 0) < Y)
                r = [jnp.where(inside, f[x], 0.0) for x in range(X)]
                p = list(r)
                answer = [jnp.zeros((Yp, L), F32) for _ in range(X)]

                def inner(u, v):
                    s = u[0] * v[0]
                    for x in range(1, X):
                        s = s + u[x] * v[x]
                    return total(s)

                rr = inner(r, r)
                for _ in range(BOTTOM_ITERS):
                    for x in range(X):
                        e[0, x + 1, 8 : 8 + Yp, :] = p[x]
                    q = [jnp.where(inside, applied(k, 0, x, False)[1], 0.0) for x in range(X)]
                    a = rr / inner(p, q)
                    answer = [u + a * v for u, v in zip(answer, p)]
                    r = [u - a * v for u, v in zip(r, q)]
                    new = inner(r, r)
                    ratio = new / rr
                    p = [u + ratio * v for u, v in zip(r, p)]
                    rr = new
                for x in range(X):
                    e[1, x + 1, 8 : 8 + Yp, :] = answer[x]
                return
            put(0, lambda x: w[x] * f[x])
            put(1, lambda x: relaxed(k, 0, x, False))
            pairs_of(k, lambda x: left(k, 1, x, False))
            R[f"f{k + 1}"][...] = coarsened(k)
            solve(k + 1)
            prolong(k)
            put(0, lambda x: e[1, x + 1, 8 : 8 + Yp, :] + kept(k, x // 2, Yp))
            put(1, lambda x: relaxed(k, 0, x, False))
            put(0, lambda x: relaxed(k, 1, x, False))

        def prolong(k):
            X, Y, Z = shapes[k]
            Yc = up_to(Y // 2, 8)
            b = 1 if k + 1 == LEVELS - 1 else 0
            C = pick(lanes[k + 1], lanes[k], lambda r, c: (c // 2 == r) & (c < Z), 1.0)
            v = R[f"e{k + 1}"][b, 1 : X // 2 + 1, 8 : 8 + Yc, :]
            v = dot(v.reshape(X // 2 * Yc, lanes[k + 1]), C).reshape(X // 2, Yc, lanes[k])
            double_rows(k, v)

        solve(LOCAL)

        k = LOCAL - 1
        Xk, Yk, Zk = shapes[k]
        C = pick(glanes, lanes[k], lambda r, c: (c // 2 + pos[2] * part[2] == r) & (c < Zk), 1.0)
        B = pick(Yk, shapes[LOCAL][1], lambda r, c: r // 2 + pos[1] * part[1] == c, 1.0)
        for j in range(Xk // 2):
            v = R[f"e{LOCAL}"][0, pos[0] * part[0] + j + 1, 8 : 8 + shapes[LOCAL][1], :]
            keep(k, j, Yk, dot(dot(B, v), C))
        produce(1, 2, lambda x: R["e1"][1, x + 1, 8 : 8 + Yk, :] + kept(1, x // 2, Yk))
        receive(1, 2)
        produce(1, 3, lambda x: relaxed(1, 2, x, True))
        receive(1, 3)

        def last_one(x, c):
            v = relaxed(1, 3, x, True)
            R["w1"][x] = v
            return c

        loop(Xk, last_one)
        C = pick(lanes[1], lanes[0], lambda r, c: (c // 2 == r) & (c < Z), 1.0)
        v = dot(R["w1"][...].reshape(Xk * Yk, lanes[1]), C).reshape(Xk, Yk, lanes[0])
        double_rows(0, v)
        produce(0, 3, lambda x: R["e0"][2, x + 1, 8 : 8 + Y, :] + kept(0, x // 2, Y))
        receive(0, 3)
        produce(0, 4, lambda x: relaxed(0, 3, x, True))
        receive(0, 4)
        produce(0, 5, lambda x: relaxed(0, 4, x, True))
        receive(0, 5)

        def image(x, sums):
            upper, lower = sums
            c, a = applied(0, 5, x, True)
            R["ap"][x] = a
            return upper + fold(R["f0"][x] * c), lower + fold(a * c)

        upper, lower = loop(X, image, (jnp.zeros((8, L), F32), jnp.zeros((8, L), F32)))
        for i in range(3):
            n, me = sizes[i], pos[i]
            R[f"qs{i}"][0:8] = upper
            R[f"qs{i}"][8:16] = lower
            sums = [
                pltpu.make_async_remote_copy(
                    src_ref=R[f"qs{i}"],
                    dst_ref=R[f"q{i}"].at[me],
                    send_sem=R["gsend"].at[2, i, d],
                    recv_sem=R["grecv"].at[2, i, d],
                    device_id={AXES[i]: lax.rem(me + d, n)},
                    device_id_type=MESH,
                )
                for d in range(1, n)
            ]
            for copy in sums:
                copy.start()
            R[f"q{i}"][me] = R[f"qs{i}"][...]
            for copy in sums:
                copy.wait_recv()
            v = R[f"q{i}"][0]
            for d in range(1, n):
                v = v + R[f"q{i}"][d]
            upper, lower = v[0:8], v[8:16]
            for copy in sums:
                copy.wait_send()
        step_length = total(upper) / total(lower)

        def finish(x, c):
            p = R["e0"][5, x + 1, 8 : 8 + Y, :]
            sol_ref[x] = sg_ref[x] + (step_length * p)[:, 0:Z]
            res_ref[x] = (R["f0"][x] - step_length * R["ap"][x])[:, 0:Z]
            return c

        loop(X, finish)
        for k, b in pending:
            for copy, sends, _ in copies(k, b):
                pl.when(sends)(copy.wait_send)
        gather_sends(0)
        gather_sends(1)

    return kernel, list(scratch.values())


def solution(mesh):
    sizes = tuple(mesh.shape[a] for a in AXES)

    def body(right_side, start_guess, reaction):
        kernel, scratch = make_kernel(sizes, right_side.shape)
        out = jax.ShapeDtypeStruct(right_side.shape, F32)
        return tuple(
            pl.pallas_call(
                kernel,
                out_shape=(out, out),
                in_specs=[pl.BlockSpec(memory_space=pltpu.VMEM)] * 3,
                out_specs=(pl.BlockSpec(memory_space=pltpu.VMEM),) * 2,
                scratch_shapes=scratch,
                compiler_params=pltpu.CompilerParams(
                    collective_id=0, has_side_effects=True, vmem_limit_bytes=60 * 2**20
                ),
                name="cg_step",
            )(right_side, start_guess, reaction)
        )

    placed = P(*AXES)
    return jax.shard_map(
        body, mesh=mesh, in_specs=(placed,) * 3, out_specs=(placed,) * 2, check_vma=False
    )
```

profile of v0, /device:TPU:1, one launch (start us, length us, event | category | flops | bytes accessed | tf_op | source)
XLA Modules:
  0.0 203.9 jit_solution(13371249931152721364)
XLA Ops:
  0.6 199.8 %cg_step.1 = (f32[48,48,48]{2,1,0:T(8,128)}, f32[48,48,48]{2,1,0:T(8,128)}) custom-call(f32[48,48,48]{2,1,0:T(8,128)} %rs_ref.1, f32[48,48,48]{2,1,0:T(8,128)} %sg_ref.1, f32[48,48,48]{2,1,0:T(8,128)} %re_ref.1), custom_call_target="tpu_custom_call" | custom-call | tf_op jit(solution)/shard_map/cg_step/pallas_call | solution.py:565
  200.4 0.0 copy-start
  200.4 2.5 %copy.7 = f32[48,48,48]{2,1,0:T(8,128)} copy(f32[48,48,48]{2,1,0:T(8,128)} %get-tuple-element.4) | data formatting | bytes 884736
  202.9 0.0 copy-done
  202.9 1.0 copy.8
Async XLA Ops:
  200.4 2.5 %copy-start = (f32[48,48,48]{2,1,0:T(8,128)S(1)}, f32[48,48,48]{2,1,0:T(8,128)}, u32[]{:S(2)}) copy-start(f32[48,48,48]{2,1,0:T(8,128)} %get-tuple-element.5) | copy-start | bytes 1327108
where the time goes:
time: 204 us
  Pallas kernels  200 us (98%)
  local copies, waits for them, and re-layouts  3.47 us (2%)
    pallas_call x1, Pallas kernels, body(): pl.pallas_call(kernel, out_shape=(out, out), in_specs=[pl.BlockSpec(memor...  200 us

commit v1 on v0

v1 whole, which is shorter than its diff:
```python
import jax
import jax.numpy as jnp
from jax import lax
from jax.experimental import pallas as pl
from jax.experimental.pallas import tpu as pltpu
from jax.sharding import PartitionSpec as P

BOTTOM_ITERS = 6
AXES = ("gx", "gy", "gz")
MESH = pl.DeviceIdType.MESH
F32 = jnp.float32
BF16 = jnp.bfloat16
DAMPING = 6.0 / 7.0
KEEP = 1.0 / 7.0
SPLIT = 3
HALO = (4, 5, 5)


def loop(n, f, carry=0, unroll=4):
    while n % unroll:
        unroll -= 1

    def step(i, c):
        for k in range(unroll):
            c = f(i * unroll + k, c)
        return c

    return lax.fori_loop(0, n // unroll, step, carry)


def iota(shape, axis):
    return lax.broadcasted_iota(jnp.int32, shape, axis)


def roll(v, shift, axis=1):
    shift = shift % v.shape[axis] if isinstance(shift, int) else shift
    return v if isinstance(shift, int) and shift == 0 else pltpu.roll(v, shift, axis)


def halves(v):
    high = v.astype(BF16)
    low = (v - high.astype(F32)).astype(BF16)
    return high, low


def picked(v, table):
    high, low = halves(v)
    return jnp.dot(high, table, preferred_element_type=F32) + jnp.dot(low, table, preferred_element_type=F32)


def total(v):
    v = jnp.sum(v, axis=0, keepdims=True)
    return jnp.sum(v, axis=1, keepdims=True)


class Level:
    def __init__(self, k, block):
        self.k = k
        self.n = block >> k
        self.h = HALO[k]
        self.r = 1 << k
        self.q = 0.25**k
        self.tiles = -(-(self.n + 2 * self.h) // 8)
        self.rows = 8 * self.tiles
        self.slabs = self.n + self.h
        self.first = 8 + self.h
        self.shape = (self.slabs + 2, self.rows + 16, 128)


def make_kernel(sizes, block):
    nx, ny, nz = sizes
    B = block[0]
    levels = [Level(k, B) for k in range(SPLIT)]
    n3 = B >> SPLIT
    groups = n3 * n3
    planes = -(-groups * 8 // 128)
    q3, q4 = 0.25**3, 0.25**4
    line = nz
    plane = nx * ny

    scratch = {}
    for name in ("rsr", "sgr", "rer"):
        scratch[name] = pltpu.VMEM((B, B, B), F32)
    scratch["insem"] = pltpu.SemaphoreType.DMA((3,))
    exchanges = {}

    def add_exchange(name, k, field, t, wide):
        lv = levels[k]
        slabs = lv.slabs if wide else lv.n
        per = 128 // (t * lv.r)
        ex = dict(name=name, lv=lv, field=field, t=t, wide=wide, slabs=slabs, per=per,
                  pairs=-(-slabs // 2), groups=-(-slabs // per))
        for d in ("s", "r"):
            scratch[f"y{d}_{name}"] = pltpu.VMEM((2, ex["pairs"], t, 128), F32)
            scratch[f"z{d}_{name}"] = pltpu.VMEM((2, ex["groups"], lv.rows, 128), F32)
        scratch[f"send_{name}"] = pltpu.SemaphoreType.DMA((5,))
        scratch[f"recv_{name}"] = pltpu.SemaphoreType.DMA((5,))
        exchanges[name] = ex

    for lv in levels:
        k = lv.k
        for name in ("f", "s", "w", "e", "a", "b"):
            scratch[f"{name}{k}"] = pltpu.VMEM(lv.shape, F32)
        scratch[f"vm{k}"] = pltpu.VMEM((lv.rows, 128), F32)
        scratch[f"t{k}"] = pltpu.VMEM((lv.n // 2, lv.rows, 128), F32)
        scratch[f"u{k}"] = pltpu.VMEM((lv.slabs // 2 + 1, lv.rows + 16, 128), F32)
        add_exchange(f"f{k}", k, f"f{k}", lv.h, True)
        add_exchange(f"s{k}", k, f"s{k}", lv.h, True)
    scratch["sg"] = pltpu.VMEM(levels[0].shape, F32)
    add_exchange("sg", 0, "sg", 1, False)
    scratch["ap"] = pltpu.VMEM((B, levels[0].rows, 128), F32)
    scratch["own"] = pltpu.VMEM((levels[0].rows, 128), F32)
    for name, count in (("gs", planes), ("gf", planes), ("gr", 2)):
        scratch[f"{name}a"] = pltpu.VMEM((plane, count, 128), F32)
        scratch[f"{name}b"] = pltpu.VMEM((count, line, plane, 128), F32)
        for m, c in (("a", plane), ("b", line)):
            scratch[f"{name}{m}_send"] = pltpu.SemaphoreType.DMA((c,))
            scratch[f"{name}{m}_recv"] = pltpu.SemaphoreType.DMA((c,))
    scratch["l3"] = pltpu.VMEM((n3, 8, 128), F32)
    for name in ("s3", "f3", "w3", "e3"):
        scratch[name] = pltpu.VMEM((planes * 128, 128), F32)
    scratch["x3"] = pltpu.VMEM((planes, plane * line, 128), F32)
    scratch["lhs"] = pltpu.VMEM((3, (n3 + 2) * 16, planes * 128), F32)

    names = list(scratch)

    def kernel(rs_ref, sg_ref, re_ref, sol_ref, res_ref, *refs):
        R = dict(zip(names, refs))
        gx, gy, gz = (lax.axis_index(a) for a in AXES)
        mine = gx * ny + gy

        inputs = [
            pltpu.make_async_copy(src, R[dst], R["insem"].at[i])
            for i, (src, dst) in enumerate(((sg_ref, "sgr"), (re_ref, "rer"), (rs_ref, "rsr")))
        ]
        for copy in inputs:
            copy.start()

        def start_of(lv):
            return 1 + gx * lv.h

        for lv in levels:
            k = lv.k
            z8 = jnp.zeros((8, 128), F32)
            zs = jnp.zeros((lv.rows, 128), F32)
            fields = ["e", "a", "b"] + (["sg"] if k == 0 else [])
            fields = [R[f if f == "sg" else f"{f}{k}"] for f in fields]

            def guard(a, c, fields=fields, lv=lv, z8=z8):
                for ref in fields:
                    ref[a, 0:8, :] = z8
                    ref[a, 8 + lv.rows : 16 + lv.rows, :] = z8
                return c

            loop(lv.shape[0], guard, 0, 2)
            for ref in fields:
                ref[0, 8 : 8 + lv.rows, :] = zs
                ref[lv.slabs + 1, 8 : 8 + lv.rows, :] = zs

            def blank(a, c, k=k, lv=lv):
                for name in ("f", "s"):
                    ref = R[f"{name}{k}"]
                    ref[a, 8:16, :] = jnp.zeros((8, 128), F32)
                    low = (lv.first + lv.n) // 8 * 8
                    ref[a, low : 8 + lv.rows, :] = jnp.zeros((8 + lv.rows - low, 128), F32)
                if k == 0:
                    ref = R["sg"]
                    ref[a, 8:16, :] = jnp.zeros((8, 128), F32)
                    ref[a, low : 8 + lv.rows, :] = jnp.zeros((8 + lv.rows - low, 128), F32)
                return c

            loop(lv.shape[0], blank, 0, 2)
            lane, row = iota((lv.rows, 128), 1), iota((lv.rows, 128), 0)
            wd = lv.h * lv.r
            ok = (lane < B) | ((lane < B + wd) & (gz < nz - 1)) | ((lane >= 128 - wd) & (gz > 0))
            ok = ok & (row >= jnp.where(gy > 0, 0, lv.h))
            ok = ok & (row < lv.n + lv.h + jnp.where(gy < ny - 1, lv.h, 0))
            R[f"vm{k}"][...] = jnp.where(ok, 1.0, 0.0)
            if k == 0:
                own = (lane < B) & (row >= lv.h) & (row < lv.h + lv.n)
                R["own"][...] = jnp.where(own, 1.0, 0.0)
        for name, ex in exchanges.items():
            for m in ("y", "z"):
                ref = R[f"{m}r_{name}"]
                side, at = (gy, ny) if m == "y" else (gz, nz)

                @pl.when((side == 0) | (side == at - 1))
                def _(ref=ref):
                    ref[...] = jnp.zeros(ref.shape, F32)

        barrier = pltpu.get_barrier_semaphore()
        others = []
        for dx in range(nx):
            for dy in range(ny):
                if dx or dy:
                    others.append({"gx": lax.rem(gx + dx, nx), "gy": lax.rem(gy + dy, ny)})
        lines = [{"gz": lax.rem(gz + d, nz)} for d in range(1, nz)]
        for to in others + lines:
            pl.semaphore_signal(barrier, inc=1, device_id=to, device_id_type=MESH)

        def part(name, i):
            ex = exchanges[name]
            lv, t = ex["lv"], ex["t"]
            f = R[ex["field"]]
            src = jnp.where(gx == 0, 1 + lv.n - t, 1 + lv.h)
            dst = jnp.where(gx == 0, 1 + lv.h - t, 1 + lv.n)
            ys, yr, zs, zr = (R[f"{m}_{name}"] for m in ("ys", "yr", "zs", "zr"))
            pairs = (
                (f.at[pl.ds(src, t), 8 : 8 + lv.rows, :], f.at[pl.ds(dst, t), 8 : 8 + lv.rows, :],
                 {"gx": 1 - gx}, None, None),
                (ys.at[0], yr.at[1], {"gy": gy - 1}, gy > 0, gy < ny - 1),
                (ys.at[1], yr.at[0], {"gy": gy + 1}, gy < ny - 1, gy > 0),
                (zs.at[0], zr.at[1], {"gz": gz - 1}, gz > 0, gz < nz - 1),
                (zs.at[1], zr.at[0], {"gz": gz + 1}, gz < nz - 1, gz > 0),
            )
            s, d, to, sends, gets = pairs[i]
            copy = pltpu.make_async_remote_copy(
                src_ref=s, dst_ref=d, send_sem=R[f"send_{name}"].at[i], recv_sem=R[f"recv_{name}"].at[i],
                device_id=to, device_id_type=MESH)
            return copy, sends, gets

        at = {"x": (0,), "y": (1, 2), "z": (3, 4)}

        def doing(cond, f):
            if cond is None:
                f()
            else:
                pl.when(cond)(f)

        def send(name, axis):
            for i in at[axis]:
                copy, sends, _ = part(name, i)
                doing(sends, copy.start)

        def arrive(name, axis):
            for i in at[axis]:
                copy, _, gets = part(name, i)
                doing(gets, copy.wait_recv)

        def sent(name, axis):
            for i in at[axis]:
                copy, sends, _ = part(name, i)
                doing(sends, copy.wait_send)

        def base(ex):
            return 1 if ex["wide"] else start_of(ex["lv"])

        def y_pack(name):
            ex = exchanges[name]
            lv, t, m = ex["lv"], ex["t"], ex["pairs"]
            f, a = R[ex["field"]], base(ex)
            lane = iota((t, 128), 1)
            for side, row in ((0, lv.first), (1, lv.first + lv.n - t)):
                for i in range(m):
                    v = f[a + i, row : row + t, :]
                    if i + m < ex["slabs"]:
                        v = jnp.where(lane < 64, v, roll(f[a + i + m, row : row + t, :], 64))
                    R[f"ys_{name}"][side, i] = v

        def y_unpack(name):
            ex = exchanges[name]
            lv, t, m = ex["lv"], ex["t"], ex["pairs"]
            f, a = R[ex["field"]], base(ex)
            lane = iota((t, 128), 1)
            for side, row in ((0, lv.first - t), (1, lv.first + lv.n)):
                for i in range(m):
                    v = R[f"yr_{name}"][side, i]
                    f[a + i, row : row + t, :] = jnp.where(lane < B, v, 0.0)
                    if i + m < ex["slabs"]:
                        f[a + i + m, row : row + t, :] = jnp.where(lane < B, roll(v, 64), 0.0)

        def z_pack(name):
            ex = exchanges[name]
            lv, per = ex["lv"], ex["per"]
            wd = ex["t"] * lv.r
            f, a = R[ex["field"]], base(ex)
            lane = iota((lv.rows, 128), 1)
            for g in range(ex["groups"]):
                low = high = None
                count = min(per, ex["slabs"] - g * per)
                for j in reversed(range(count)):
                    v = f[a + g * per + j, 8 : 8 + lv.rows, :]
                    c = j * wd
                    one, two = roll(v, c), roll(v, c - (B - wd))
                    low = one if low is None else jnp.where(lane < c + wd, one, low)
                    high = two if high is None else jnp.where(lane < c + wd, two, high)
                R[f"zs_{name}"][0, g] = low
                R[f"zs_{name}"][1, g] = high

        def z_unpacked(name, use):
            ex = exchanges[name]
            lv, per = ex["lv"], ex["per"]
            wd = ex["t"] * lv.r
            f, a = R[ex["field"]], base(ex)
            lane = iota((lv.rows, 128), 1)
            for g in range(ex["groups"]):
                count = min(per, ex["slabs"] - g * per)
                for j in range(count):
                    i = a + g * per + j
                    c = j * wd
                    below = roll(R[f"zr_{name}"][0, g], -wd - c)
                    above = roll(R[f"zr_{name}"][1, g], B - c)
                    v = jnp.where(lane < B + wd, above, jnp.where(lane >= 128 - wd, below, 0.0))
                    use(i, jnp.where(lane < B, f[i, 8 : 8 + lv.rows, :], v))

        def beside_of(lv, ref, a):
            rows = lv.rows
            c = ref[a, 8 : 8 + rows, :]
            v = ref[a + 1, 8 : 8 + rows, :] + ref[a - 1, 8 : 8 + rows, :]
            v = v + (ref[a, 9 : 9 + rows, :] + ref[a, 7 : 7 + rows, :])
            return c, v + (roll(c, lv.r) + roll(c, -lv.r))

        def span(lv, far):
            return lv.n + far, 1 + gx * (lv.h - far)

        def relax(lv, src, dst, far, unroll=2):
            k = lv.k
            count, a0 = span(lv, far)

            def one(i, carry):
                a = a0 + i
                c, v = beside_of(lv, R[f"{src}{k}"], a)
                w = R[f"w{k}"][a, 8 : 8 + lv.rows, :]
                e = R[f"e{k}"][a, 8 : 8 + lv.rows, :]
                R[f"{dst}{k}"][a, 8 : 8 + lv.rows, :] = c * KEEP + (e + w * v)
                return carry

            loop(count, one, 0, unroll)

        def weigh(lv):
            k = lv.k
            vm = R[f"vm{k}"]

            def use(i, s):
                R[f"w{k}"][i, 8 : 8 + lv.rows, :] = vm[...] * ((DAMPING * lv.q) / (6.0 * lv.q + s))

            z_unpacked(f"s{k}", use)

        def begin(lv):
            k = lv.k
            scale = 1.0 / lv.q

            def use(i, f):
                w = R[f"w{k}"][i, 8 : 8 + lv.rows, :]
                R[f"e{k}"][i, 8 : 8 + lv.rows, :] = (w * scale) * f if k else w * f

            z_unpacked(f"f{k}", use)

        def restrict(lv, of, name):
            k = lv.k
            a0 = start_of(lv)
            half = lv.n // 2
            lane = iota((lv.rows, 128), 1)
            t = R[f"t{k}"]

            def one(j, c):
                v = of(a0 + 2 * j) + of(a0 + 2 * j + 1)
                v = v + jnp.where((lane & lv.r) == 0, roll(v, -lv.r), roll(v, lv.r))
                t[j] = v
                return c

            loop(half, one, 0, 2)
            wide = iota((half, 128), 1) < B

            def two(j, c):
                v = t[j, pl.ds(lv.h, half, stride=2), :] + t[j, pl.ds(lv.h + 1, half, stride=2), :]
                v = jnp.where(wide, 0.125 * v, 0.0)
                if k + 1 < SPLIT:
                    nxt = levels[k + 1]
                    R[f"{name}{k + 1}"][start_of(nxt) + j, nxt.first : nxt.first + half, :] = v
                else:
                    R["l3"][j, 0:half, :] = v
                return c

            loop(half, two, 0, 2)

        def left_of(lv, src):
            k = lv.k

            def f(a):
                c, v = beside_of(lv, R[f"{src}{k}"], a)
                s = R[f"s{k}"][a, 8 : 8 + lv.rows, :]
                return R[f"f{k}"][a, 8 : 8 + lv.rows, :] - ((6.0 * lv.q + s) * c - lv.q * v)

            return f

        def coefficient(lv):
            return lambda a: R[f"s{lv.k}"][a, 8 : 8 + lv.rows, :]

        def prolong(lv, coarse_rows):
            k = lv.k
            nxt_far = 2
            half = lv.n // 2
            m = half + 2 * nxt_far
            shift = lv.h - 2 * nxt_far
            u = R[f"u{k}"]

            def put(j, c):
                v = coarse_rows(j, m)
                u[j, pl.ds(shift, m, stride=2), :] = v
                u[j, pl.ds(shift + 1, m, stride=2), :] = v
                return c

            loop(half + nxt_far, put, 0, 2)

        def add_up(lv):
            k = lv.k
            a0 = 1 + gx * (lv.h - 4)

            def one(j, c):
                p = R[f"u{k}"][j, 0 : lv.rows, :]
                if k:
                    row = iota((lv.rows, 128), 0)
                    p = jnp.where((row >= lv.h - 4) & (row < lv.h + lv.n + 4), p, 0.0)
                if k == SPLIT - 1:
                    p = jnp.where(R[f"vm{k}"][...] > 0.0, p, 0.0)
                for d in range(2):
                    a = a0 + 2 * j + d
                    R[f"b{k}"][a, 8 : 8 + lv.rows, :] = R[f"a{k}"][a, 8 : 8 + lv.rows, :] + p
                return c

            loop((lv.n + 4) // 2, one, 0, 2)

        def gather_a(name):
            a = R[f"{name}a"]
            out = []
            for d, to in enumerate(others):
                out.append(pltpu.make_async_remote_copy(
                    src_ref=a.at[mine], dst_ref=a.at[mine], send_sem=R[f"{name}a_send"].at[d],
                    recv_sem=R[f"{name}a_recv"].at[d], device_id=to, device_id_type=MESH))
            return out

        def gather_b(name):
            b = R[f"{name}b"]
            out = []
            for d, to in enumerate(lines):
                out.append(pltpu.make_async_remote_copy(
                    src_ref=b.at[:, gz], dst_ref=b.at[:, gz], send_sem=R[f"{name}b_send"].at[d],
                    recv_sem=R[f"{name}b_recv"].at[d], device_id=to, device_id_type=MESH))
            return out

        def gather_start(name, rows):
            for p, v in enumerate(rows):
                R[f"{name}a"][mine, p : p + 1, :] = v
            for copy in gather_a(name):
                copy.start()

        def gather_middle(name, count):
            for copy in gather_a(name):
                copy.wait_recv()
            for p in range(count):
                for j in range(plane):
                    R[f"{name}b"][p, gz, j : j + 1, :] = R[f"{name}a"][j, p : p + 1, :]
            for copy in gather_b(name):
                copy.start()

        def gather_end(name):
            for copy in gather_b(name):
                copy.wait_recv()

        def gather_sent(name):
            for copy in gather_a(name) + gather_b(name):
                copy.wait_send()

        def local_vector():
            wide = planes * 128
            v = R["l3"][...].reshape(n3 * 8, 128)
            l, c = iota((128, wide), 0), iota((128, wide), 1)
            table = jnp.where((l == (c & 7) * (1 << SPLIT)) & ((c & 7) < n3) & (c < groups * 8), 1.0, 0.0).astype(BF16)
            v = picked(v, table)
            row, c = iota((n3 * 8, wide), 0), iota((n3 * 8, wide), 1)
            keep = ((row & 7) < n3) & ((c >> 3) == (row >> 3) * n3 + (row & 7))
            v = jnp.sum(jnp.where(keep, v, 0.0), axis=0, keepdims=True)
            return [v[:, 128 * p : 128 * p + 128] for p in range(planes)]

        def by_device(name, dst):
            for p in range(planes):
                v = R[f"{name}b"][p].reshape(plane * line, 128)
                R[dst][128 * p : 128 * p + 128, :] = v.T

        lv0, lv1, lv2 = levels
        inside = jnp.zeros((B, 128 - B), F32)

        def take(raw, dst):
            def one(x, c):
                v = jnp.concatenate([R[raw][x], inside], axis=1)
                R[dst][start_of(lv0) + x, lv0.first : lv0.first + B, :] = v
                return c

            loop(B, one, 0, 4)

        R["l3"][...] = jnp.zeros((n3, 8, 128), F32)
        inputs[0].wait()
        take("sgr", "sg")
        y_pack("sg")
        z_pack("sg")
        pl.semaphore_wait(barrier, len(others) + len(lines))
        for axis in "xyz":
            send("sg", axis)
        inputs[1].wait()
        take("rer", "s0")
        send("s0", "x")
        inputs[2].wait()
        take("rsr", "f0")
        restrict(lv0, coefficient(lv0), "s")
        send("s1", "x")
        restrict(lv1, coefficient(lv1), "s")
        send("s2", "x")
        restrict(lv2, coefficient(lv2), "s")
        gather_start("gs", local_vector())
        arrive("s0", "x")
        y_pack("s0")
        send("s0", "y")

        for axis in "xyz":
            arrive("sg", axis)
        sent("sg", "x")
        y_unpack("sg")

        def keep_guess(i, v):
            R["sg"][i, 8 : 8 + lv0.rows, :] = v

        z_unpacked("sg", keep_guess)

        def first_residual(x, carry):
            a = start_of(lv0) + x
            c, v = beside_of(lv0, R["sg"], a)
            s = R["s0"][a, 8 : 8 + lv0.rows, :]
            f = R["f0"][a, 8 : 8 + lv0.rows, :] - ((6.0 + s) * c - v)
            R["f0"][a, 8 : 8 + lv0.rows, :] = jnp.where(R["own"][...] > 0.0, f, 0.0)
            return carry

        loop(B, first_residual, 0, 2)
        send("f0", "x")
        for k in (1, 2):
            arrive(f"s{k}", "x")
            y_pack(f"s{k}")
            send(f"s{k}", "y")
        arrive("s0", "y")
        sent("s0", "x")
        y_unpack("s0")
        z_pack("s0")
        arrive("f0", "x")
        y_pack("f0")
        send("f0", "y")
        send("s0", "z")
        gather_middle("gs", planes)
        arrive("f0", "y")
        sent("f0", "x")
        y_unpack("f0")
        z_pack("f0")
        send("f0", "z")
        for k in (1, 2):
            arrive(f"s{k}", "y")
            sent(f"s{k}", "x")
            y_unpack(f"s{k}")
            z_pack(f"s{k}")
            send(f"s{k}", "z")
        arrive("s0", "z")
        weigh(lv0)
        arrive("f0", "z")

        begin(lv0)

        def first_relax(lv):
            k = lv.k
            count, a0 = span(lv, 4)

            def one(i, carry):
                a = a0 + i
                c, v = beside_of(lv, R[f"e{k}"], a)
                w = R[f"w{k}"][a, 8 : 8 + lv.rows, :]
                R[f"a{k}"][a, 8 : 8 + lv.rows, :] = c * (1.0 + KEEP) + w * v
                return carry

            loop(count, one, 0, 2)

        first_relax(lv0)
        restrict(lv0, left_of(lv0, "a"), "f")

        def deeper(lv, fill):
            k = lv.k
            name = f"f{k}"
            send(name, "x")
            fill()
            arrive(name, "x")
            y_pack(name)
            send(name, "y")
            arrive(name, "y")
            sent(name, "x")
            y_unpack(name)
            z_pack(name)
            send(name, "z")
            arrive(f"s{k}", "z")
            weigh(lv)
            arrive(name, "z")
            begin(lv)
            first_relax(lv)
            restrict(lv, left_of(lv, "a"), "f")

        deeper(lv1, lambda: None)
        deeper(lv2, lambda: None)
        gather_start("gf", local_vector())

        gather_end("gs")
        by_device("gs", "s3")
        lane8, row8 = iota((8, 128), 1), iota((8, 128), 0)
        dev_y, dev_x, dev_z = lane8 & (ny - 1), (lane8 >> 2) & 1, lane8 >> 3
        step_x, step_z = ny, plane
        has = {
            ("y", 1): dev_y < ny - 1, ("y", -1): dev_y > 0, ("x", 1): dev_x < nx - 1, ("x", -1): dev_x > 0,
            ("z", 1): dev_z < nz - 1, ("z", -1): dev_z > 0,
        }
        strides = {"y": 1, "x": step_x, "z": step_z}

        def across(v, axis, way):
            return jnp.where(has[axis, way], roll(v, -way * strides[axis]), 0.0)

        def around(get, m):
            def one(x, y):
                c = get(x, y)
                r = n3 // m
                up = jnp.where(row8 >= n3 - r, roll(across(c, "z", 1), n3 - r, 0), roll(c, -r, 0))
                dn = jnp.where(row8 < r, roll(across(c, "z", -1), r - n3, 0), roll(c, r, 0))
                v = up + dn
                v = v + (get(x + 1, y) if x + 1 < m else across(get(0, y), "x", 1))
                v = v + (get(x - 1, y) if x else across(get(m - 1, y), "x", -1))
                v = v + (get(x, y + 1) if y + 1 < m else across(get(x, 0), "y", 1))
                v = v + (get(x, y - 1) if y else across(get(x, m - 1), "y", -1))
                return c, v

            return one

        cells = [(x, y) for x in range(n3) for y in range(n3)]
        m4 = n3 // 2
        cells4 = [(x, y) for x in range(m4) for y in range(m4)]
        live = row8 < n3

        def tile(name, x, y):
            g = x * n3 + y
            return R[name][8 * g : 8 * g + 8, :]

        for x, y in cells:
            R["w3"][8 * (x * n3 + y) : 8 * (x * n3 + y) + 8, :] = jnp.where(
                live, (DAMPING * q3) / (6.0 * q3 + tile("s3", x, y)), 0.0)

        def coarser(get):
            out = {}
            for x, y in cells4:
                v = (get(2 * x, 2 * y) + get(2 * x, 2 * y + 1)) + (get(2 * x + 1, 2 * y) + get(2 * x + 1, 2 * y + 1))
                v = v + jnp.where((row8 & 1) == 0, roll(v, -1, 0), roll(v, 1, 0))
                out[x, y] = jnp.where(live, 0.125 * v, 0.0)
            return out

        s4 = coarser(lambda x, y: tile("s3", x, y))
        gather_middle("gf", planes)
        gather_end("gf")
        by_device("gf", "f3")
        e = {}
        e0 = {}
        for c in cells:
            e0[c] = (tile("w3", *c) * (1.0 / q3)) * tile("f3", *c)
        op = around(lambda x, y: e0[x, y], n3)
        for c in cells:
            u, v = op(*c)
            e[c] = u * (1.0 + KEEP) + tile("w3", *c) * v
        op = around(lambda x, y: e[x, y], n3)
        rest = {}
        for c in cells:
            u, v = op(*c)
            rest[c] = jnp.where(live, tile("f3", *c) - ((6.0 * q3 + tile("s3", *c)) * u - q3 * v), 0.0)
        f4 = coarser(lambda x, y: rest[x, y])

        def inner(u, v):
            s = None
            for c in cells4:
                s = u[c] * v[c] if s is None else s + u[c] * v[c]
            return total(s)

        r4 = dict(f4)
        p4 = dict(f4)
        e4 = {c: jnp.zeros((8, 128), F32) for c in cells4}
        rr = inner(r4, r4)
        for _ in range(BOTTOM_ITERS):
            op = around(lambda x, y: p4[x, y], m4)
            q = {}
            for c in cells4:
                u, v = op(*c)
                q[c] = jnp.where(live, (6.0 * q4 + s4[c]) * u - q4 * v, 0.0)
            a = rr / inner(p4, q)
            e4 = {c: e4[c] + a * p4[c] for c in cells4}
            r4 = {c: r4[c] - a * q[c] for c in cells4}
            new = inner(r4, r4)
            ratio = new / rr
            p4 = {c: r4[c] + ratio * p4[c] for c in cells4}
            rr = new
        e = {(x, y): e[x, y] + e4[x // 2, y // 2] for x, y in cells}
        for _ in range(2):
            op = around(lambda x, y: e[x, y], n3)
            nxt = {}
            for c in cells:
                u, v = op(*c)
                nxt[c] = u * KEEP + (e0[c] + tile("w3", *c) * v)
            e = nxt
        for x, y in cells:
            g = x * n3 + y
            R["e3"][8 * g : 8 * g + 8, :] = e[x, y]
        R["e3"][groups * 8 :, :] = jnp.zeros((planes * 128 - groups * 8, 128), F32)
        for p in range(planes):
            R["x3"][p] = R["e3"][128 * p : 128 * p + 128, :].T

        wide = planes * 128
        slabs3 = n3 + 2
        lane_w = iota((8, wide), 1) >> 3
        row_w = iota((8, wide), 0)
        lo_rows = jnp.where(row_w < 2, n3 - 2 + row_w, -1000)
        mid_rows = jnp.where(row_w < 2, -1000, row_w - 2)
        hi_rows = jnp.where(row_w < 2, row_w, -1000)
        y_below, y_above = jnp.maximum(gy - 1, 0), jnp.minimum(gy + 1, ny - 1)
        z_at = [jnp.maximum(gz - 1, 0), gz, jnp.minimum(gz + 1, nz - 1)]

        def vector(dev):
            return jnp.concatenate([R["x3"][p, pl.ds(dev, 1), :] for p in range(planes)], axis=1)

        for i in range(slabs3):
            partner = jnp.where(gx == 0, i >= n3, i < 2)
            px = jnp.where(partner, 1 - gx, gx)
            xx = jnp.where(gx == 0, i - jnp.where(i >= n3, n3, 0), i - 2 + jnp.where(i < 2, n3, 0))
            lo, mid, hi = (lane_w == xx * n3 + rows for rows in (lo_rows, mid_rows, hi_rows))
            for d in range(3):
                at_y = lambda g: vector(z_at[d] * plane + px * ny + g)
                first = jnp.where(mid, at_y(gy), jnp.where(lo, at_y(y_below), 0.0))
                second = jnp.where(hi, at_y(y_above), 0.0)
                R["lhs"][d, 16 * i : 16 * i + 8, :] = first
                R["lhs"][d, 16 * i + 8 : 16 * i + 16, :] = second
        l, c = iota((wide, 128), 1), iota((wide, 128), 0)
        table = jnp.where((l < B) & ((c & 7) == (l >> SPLIT)) & (c < groups * 8), 1.0, 0.0).astype(BF16)
        v = picked(R["lhs"][...].reshape(3 * slabs3 * 16, wide), table).reshape(3, slabs3, 16, 128)
        v = v[1] + roll(v[2].reshape(slabs3 * 16, 128), B).reshape(slabs3, 16, 128) + roll(
            v[0].reshape(slabs3 * 16, 128), -B).reshape(slabs3, 16, 128)
        u = R["u2"]
        shift = lv2.h - 4
        for i in range(slabs3):
            m = n3 + 4
            u[i, pl.ds(shift, m, stride=2), :] = v[i, 0:m]
            u[i, pl.ds(shift + 1, m, stride=2), :] = v[i, 0:m]

        add_up(lv2)
        relax(lv2, "b", "a", 4)
        relax(lv2, "a", "b", 2)

        def coarse_of(nxt, ref):
            a0 = 1 + gx * (nxt.h - 2)
            return lambda j, m: R[ref][a0 + j, nxt.first - 2 : nxt.first - 2 + m, :]

        prolong(lv1, coarse_of(lv2, "b2"))
        add_up(lv1)
        relax(lv1, "b", "a", 4)
        relax(lv1, "a", "b", 2)
        prolong(lv0, coarse_of(lv1, "b1"))
        add_up(lv0)
        relax(lv0, "b", "a", 4)
        relax(lv0, "a", "b", 2)

        def image(x, sums):
            upper, lower = sums
            a = start_of(lv0) + x
            c, v = beside_of(lv0, R["b0"], a)
            s = R["s0"][a, 8 : 8 + lv0.rows, :]
            ap = (6.0 + s) * c - v
            R["ap"][x] = ap
            c = jnp.where(R["own"][...] > 0.0, c, 0.0)
            return upper + R["f0"][a, 8 : 8 + lv0.rows, :] * c, lower + ap * c

        zero = jnp.zeros((lv0.rows, 128), F32)
        upper, lower = loop(B, image, (zero, zero), 2)
        gather_start("gr", [jnp.sum(v, axis=0, keepdims=True) for v in (upper, lower)])
        gather_middle("gr", 2)
        gather_end("gr")
        sums = [total(jnp.sum(R["grb"][p], axis=0)) for p in range(2)]
        step_length = sums[0] / sums[1]

        def finish(x, c):
            a = start_of(lv0) + x
            p = R["b0"][a, lv0.first : lv0.first + B, :]
            f = R["f0"][a, lv0.first : lv0.first + B, :]
            q = R["ap"][x, lv0.h : lv0.h + B, :]
            sol_ref[x] = R["sgr"][x] + (step_length * p)[:, 0:B]
            res_ref[x] = (f - step_length * q)[:, 0:B]
            return c

        loop(B, finish, 0, 2)
        for name in exchanges:
            for axis in "yz":
                sent(name, axis)
        for name in ("gs", "gf", "gr"):
            gather_sent(name)

    return kernel, list(scratch.values())


def solution(mesh):
    sizes = tuple(mesh.shape[a] for a in AXES)

    def body(right_side, start_guess, reaction):
        kernel, scratch = make_kernel(sizes, right_side.shape)
        out = jax.ShapeDtypeStruct(right_side.shape, F32)
        return tuple(
            pl.pallas_call(
                kernel,
                out_shape=(out, out),
                in_specs=[pl.BlockSpec(memory_space=pl.ANY)] * 3,
                out_specs=(pl.BlockSpec(memory_space=pltpu.VMEM),) * 2,
                scratch_shapes=scratch,
                compiler_params=pltpu.CompilerParams(
                    collective_id=0, has_side_effects=True, vmem_limit_bytes=60 * 2**20
                ),
                name="cg_step",
            )(right_side, start_guess, reaction)
        )

    placed = P(*AXES)
    return jax.shard_map(
        body, mesh=mesh, in_specs=(placed,) * 3, out_specs=(placed,) * 2, check_vma=False
    )
```

time: 204 us -> 94.2 us (0.46)
  Pallas kernels: 200 us -> 90 us
    pallas_call x1, Pallas kernels: 200 us -> 90 us  [body(): pl.pallas_call(kernel, out_shape=(out, out), in_specs=[pl.BlockSpec(memor...]
where the time goes in v1:
time: 94.2 us; the launch traced here: 94.1 us
  Pallas kernels  90 us (96%)
  local copies, waits for them, and re-layouts  3.47 us (4%)
    pallas_call x1, Pallas kernels, body(): pl.pallas_call(kernel, out_shape=(out, out), in_specs=[pl.BlockSpec(memor...  90 us
    unnamed x4, local copies, waits for them, and re-layouts  3.47 us

profile of v1, /device:TPU:1, one launch (start us, length us, event | category | flops | bytes accessed | tf_op | source)
XLA Modules:
  0.0 94.1 jit_solution(11283574996770531466)
XLA Ops:
  0.6 90.0 %cg_step.1 = (f32[48,48,48]{2,1,0:T(8,128)}, f32[48,48,48]{2,1,0:T(8,128)}) custom-call(f32[48,48,48]{2,1,0:T(8,128)} %rs_ref.1, f32[48,48,48]{2,1,0:T(8,128)} %sg_ref.1, f32[48,48,48]{2,1,0:T(8,128)} %re_ref.1), custom_call_target="tpu_custom_call" | custom-call | tf_op jit(solution)/shard_map/cg_step/pallas_call | solution.py:809
  90.6 0.0 copy-start
  90.6 2.5 %copy.7 = f32[48,48,48]{2,1,0:T(8,128)} copy(f32[48,48,48]{2,1,0:T(8,128)} %get-tuple-element.4) | data formatting | bytes 884736
  93.1 0.0 copy-done
  93.1 1.0 %copy.8 = f32[48,48,48]{2,1,0:T(8,128)} copy(f32[48,48,48]{2,1,0:T(8,128)S(1)} %copy-done) | data formatting | bytes 884736
Async XLA Ops:
  90.6 2.5 %copy-start = (f32[48,48,48]{2,1,0:T(8,128)S(1)}, f32[48,48,48]{2,1,0:T(8,128)}, u32[]{:S(2)}) copy-start(f32[48,48,48]{2,1,0:T(8,128)} %get-tuple-element.5) | copy-start | bytes 1327108

commit v2 on v1

--- a/solution.py
+++ b/solution.py
@@ -17,6 +17,7 @@
 
 
 def loop(n, f, carry=0, unroll=4):
+    unroll = min(unroll, n)
     while n % unroll:
         unroll -= 1
 
@@ -64,6 +65,7 @@
         self.rows = 8 * self.tiles
         self.slabs = self.n + self.h
         self.first = 8 + self.h
+        self.unroll = 14 if k == 0 else 28
         self.shape = (self.slabs + 2, self.rows + 16, 128)
 
 
@@ -86,15 +88,17 @@
 
     def add_exchange(name, k, field, t, wide):
         lv = levels[k]
-        slabs = lv.slabs if wide else lv.n
         per = 128 // (t * lv.r)
-        ex = dict(name=name, lv=lv, field=field, t=t, wide=wide, slabs=slabs, per=per,
-                  pairs=-(-slabs // 2), groups=-(-slabs // per))
+        ex = dict(lv=lv, field=field, t=t, wide=wide, per=per, pairs=lv.n // 2, groups=-(-lv.n // per))
         for d in ("s", "r"):
             scratch[f"y{d}_{name}"] = pltpu.VMEM((2, ex["pairs"], t, 128), F32)
             scratch[f"z{d}_{name}"] = pltpu.VMEM((2, ex["groups"], lv.rows, 128), F32)
-        scratch[f"send_{name}"] = pltpu.SemaphoreType.DMA((5,))
-        scratch[f"recv_{name}"] = pltpu.SemaphoreType.DMA((5,))
+        if wide:
+            scratch[f"yx_{name}"] = pltpu.VMEM((2, t, t, 128), F32)
+            scratch[f"zx_{name}"] = pltpu.VMEM((2, lv.rows, 128), F32)
+        count = 17 if wide else 5
+        scratch[f"send_{name}"] = pltpu.SemaphoreType.DMA((count,))
+        scratch[f"recv_{name}"] = pltpu.SemaphoreType.DMA((count,))
         exchanges[name] = ex
 
     for lv in levels:
@@ -111,11 +115,9 @@
     scratch["ap"] = pltpu.VMEM((B, levels[0].rows, 128), F32)
     scratch["own"] = pltpu.VMEM((levels[0].rows, 128), F32)
     for name, count in (("gs", planes), ("gf", planes), ("gr", 2)):
-        scratch[f"{name}a"] = pltpu.VMEM((plane, count, 128), F32)
-        scratch[f"{name}b"] = pltpu.VMEM((count, line, plane, 128), F32)
-        for m, c in (("a", plane), ("b", line)):
-            scratch[f"{name}{m}_send"] = pltpu.SemaphoreType.DMA((c,))
-            scratch[f"{name}{m}_recv"] = pltpu.SemaphoreType.DMA((c,))
+        scratch[name] = pltpu.VMEM((count, line, plane, 128), F32)
+        scratch[f"{name}_send"] = pltpu.SemaphoreType.DMA((line,))
+        scratch[f"{name}_recv"] = pltpu.SemaphoreType.DMA((line,))
     scratch["l3"] = pltpu.VMEM((n3, 8, 128), F32)
     for name in ("s3", "f3", "w3", "e3"):
         scratch[name] = pltpu.VMEM((planes * 128, 128), F32)
@@ -180,104 +182,113 @@
                 own = (lane < B) & (row >= lv.h) & (row < lv.h + lv.n)
                 R["own"][...] = jnp.where(own, 1.0, 0.0)
         for name, ex in exchanges.items():
-            for m in ("y", "z"):
-                ref = R[f"{m}r_{name}"]
-                side, at = (gy, ny) if m == "y" else (gz, nz)
-
-                @pl.when((side == 0) | (side == at - 1))
-                def _(ref=ref):
-                    ref[...] = jnp.zeros(ref.shape, F32)
+            for m in ("yr", "zr") + (("yx", "zx") if ex["wide"] else ()):
+                ref = R[f"{m}_{name}"]
+                ref[...] = jnp.zeros(ref.shape, F32)
 
         barrier = pltpu.get_barrier_semaphore()
         others = []
-        for dx in range(nx):
-            for dy in range(ny):
-                if dx or dy:
-                    others.append({"gx": lax.rem(gx + dx, nx), "gy": lax.rem(gy + dy, ny)})
-        lines = [{"gz": lax.rem(gz + d, nz)} for d in range(1, nz)]
-        for to in others + lines:
-            pl.semaphore_signal(barrier, inc=1, device_id=to, device_id_type=MESH)
-
-        def part(name, i):
+        for dz in range(nz):
+            for dx in range(nx):
+                for dy in range(ny):
+                    if dx or dy or dz:
+                        others.append((dx, dy, dz))
+
+        def device(dx, dy, dz):
+            return {"gx": lax.rem(gx + dx, nx), "gy": lax.rem(gy + dy, ny), "gz": lax.rem(gz + dz, nz)}
+
+        for to in others:
+            pl.semaphore_signal(barrier, inc=1, device_id=device(*to), device_id_type=MESH)
+
+        def exists(at, n, way):
+            return at > 0 if way < 0 else at < n - 1
+
+        def messages(name):
             ex = exchanges[name]
-            lv, t = ex["lv"], ex["t"]
+            lv, t, m = ex["lv"], ex["t"], ex["pairs"]
             f = R[ex["field"]]
             src = jnp.where(gx == 0, 1 + lv.n - t, 1 + lv.h)
             dst = jnp.where(gx == 0, 1 + lv.h - t, 1 + lv.n)
-            ys, yr, zs, zr = (R[f"{m}_{name}"] for m in ("ys", "yr", "zs", "zr"))
-            pairs = (
-                (f.at[pl.ds(src, t), 8 : 8 + lv.rows, :], f.at[pl.ds(dst, t), 8 : 8 + lv.rows, :],
-                 {"gx": 1 - gx}, None, None),
-                (ys.at[0], yr.at[1], {"gy": gy - 1}, gy > 0, gy < ny - 1),
-                (ys.at[1], yr.at[0], {"gy": gy + 1}, gy < ny - 1, gy > 0),
-                (zs.at[0], zr.at[1], {"gz": gz - 1}, gz > 0, gz < nz - 1),
-                (zs.at[1], zr.at[0], {"gz": gz + 1}, gz < nz - 1, gz > 0),
-            )
-            s, d, to, sends, gets = pairs[i]
-            copy = pltpu.make_async_remote_copy(
-                src_ref=s, dst_ref=d, send_sem=R[f"send_{name}"].at[i], recv_sem=R[f"recv_{name}"].at[i],
-                device_id=to, device_id_type=MESH)
-            return copy, sends, gets
-
-        at = {"x": (0,), "y": (1, 2), "z": (3, 4)}
-
-        def doing(cond, f):
-            if cond is None:
-                f()
-            else:
-                pl.when(cond)(f)
-
-        def send(name, axis):
-            for i in at[axis]:
-                copy, sends, _ = part(name, i)
-                doing(sends, copy.start)
-
-        def arrive(name, axis):
-            for i in at[axis]:
-                copy, _, gets = part(name, i)
-                doing(gets, copy.wait_recv)
-
-        def sent(name, axis):
-            for i in at[axis]:
-                copy, sends, _ = part(name, i)
-                doing(sends, copy.wait_send)
-
-        def base(ex):
-            return 1 if ex["wide"] else start_of(ex["lv"])
+            rows = pl.ds(lv.first, lv.n)
+            own = pl.ds(lv.h, lv.n)
+            ys, yr, zs, zr = (R[f"{c}_{name}"] for c in ("ys", "yr", "zs", "zr"))
+            out = [(f.at[pl.ds(src, t), rows, :], f.at[pl.ds(dst, t), rows, :], 1, 0, 0)]
+            for i, way in enumerate((-1, 1)):
+                out.append((ys.at[i], yr.at[1 - i], 0, way, 0))
+                out.append((zs.at[i, :, own, :], zr.at[1 - i, :, own, :], 0, 0, way))
+            if ex["wide"]:
+                yx, zx = R[f"yx_{name}"], R[f"zx_{name}"]
+                pair = jnp.where(gx == 0, m - t, 0)
+                group = jnp.where(gx == 0, ex["groups"] - 1, 0)
+                for i, way in enumerate((-1, 1)):
+                    out.append((ys.at[i, pl.ds(pair, t)], yx.at[1 - i], 1, way, 0))
+                    out.append((zs.at[i, group, own, :], zx.at[1 - i, own, :], 1, 0, way))
+                    for yway in (-1, 1):
+                        here = pl.ds(lv.h if yway < 0 else lv.h + lv.n - t, t)
+                        there = pl.ds(lv.h + lv.n if yway < 0 else lv.h - t, t)
+                        out.append((zs.at[i, :, here, :], zr.at[1 - i, :, there, :], 0, yway, way))
+                        out.append((zs.at[i, group, here, :], zx.at[1 - i, there, :], 1, yway, way))
+            return out
+
+        def each(name, f, getting):
+            for i, (s, d, ox, oy, oz) in enumerate(messages(name)):
+                copy = pltpu.make_async_remote_copy(
+                    src_ref=s, dst_ref=d, send_sem=R[f"send_{name}"].at[i], recv_sem=R[f"recv_{name}"].at[i],
+                    device_id={"gx": lax.rem(gx + ox, nx), "gy": gy + oy, "gz": gz + oz}, device_id_type=MESH)
+                cond = None
+                for at, n, way in ((gy, ny, oy), (gz, nz, oz)):
+                    if way:
+                        there = exists(at, n, -way if getting else way)
+                        cond = there if cond is None else cond & there
+                if cond is None:
+                    f(copy)
+                else:
+                    pl.when(cond)(lambda copy=copy: f(copy))
+
+        def send(name):
+            each(name, lambda copy: copy.start(), False)
+
+        def arrive(name):
+            each(name, lambda copy: copy.wait_recv(), True)
+
+        def sent(name):
+            each(name, lambda copy: copy.wait_send(), False)
 
         def y_pack(name):
             ex = exchanges[name]
             lv, t, m = ex["lv"], ex["t"], ex["pairs"]
-            f, a = R[ex["field"]], base(ex)
+            f, a = R[ex["field"]], start_of(lv)
             lane = iota((t, 128), 1)
             for side, row in ((0, lv.first), (1, lv.first + lv.n - t)):
                 for i in range(m):
                     v = f[a + i, row : row + t, :]
-                    if i + m < ex["slabs"]:
-                        v = jnp.where(lane < 64, v, roll(f[a + i + m, row : row + t, :], 64))
-                    R[f"ys_{name}"][side, i] = v
+                    R[f"ys_{name}"][side, i] = jnp.where(lane < 64, v, roll(f[a + i + m, row : row + t, :], 64))
 
         def y_unpack(name):
             ex = exchanges[name]
             lv, t, m = ex["lv"], ex["t"], ex["pairs"]
-            f, a = R[ex["field"]], base(ex)
-            lane = iota((t, 128), 1)
+            f, a = R[ex["field"]], start_of(lv)
+            keep = iota((t, 128), 1) < B
+            edge = jnp.where(gx == 0, 1 + lv.n, 1)
             for side, row in ((0, lv.first - t), (1, lv.first + lv.n)):
                 for i in range(m):
                     v = R[f"yr_{name}"][side, i]
-                    f[a + i, row : row + t, :] = jnp.where(lane < B, v, 0.0)
-                    if i + m < ex["slabs"]:
-                        f[a + i + m, row : row + t, :] = jnp.where(lane < B, roll(v, 64), 0.0)
+                    f[a + i, row : row + t, :] = jnp.where(keep, v, 0.0)
+                    f[a + i + m, row : row + t, :] = jnp.where(keep, roll(v, 64), 0.0)
+                if ex["wide"]:
+                    for i in range(t):
+                        v = pltpu.roll(R[f"yx_{name}"][side, i], gx * 64, 1)
+                        f[edge + i, row : row + t, :] = jnp.where(keep, v, 0.0)
 
         def z_pack(name):
             ex = exchanges[name]
             lv, per = ex["lv"], ex["per"]
             wd = ex["t"] * lv.r
-            f, a = R[ex["field"]], base(ex)
+            f, a = R[ex["field"]], start_of(lv)
             lane = iota((lv.rows, 128), 1)
             for g in range(ex["groups"]):
                 low = high = None
-                count = min(per, ex["slabs"] - g * per)
+                count = min(per, lv.n - g * per)
                 for j in reversed(range(count)):
                     v = f[a + g * per + j, 8 : 8 + lv.rows, :]
                     c = j * wd
@@ -287,21 +298,32 @@
                 R[f"zs_{name}"][0, g] = low
                 R[f"zs_{name}"][1, g] = high
 
+        def pack_send(name):
+            y_pack(name)
+            z_pack(name)
+            send(name)
+
         def z_unpacked(name, use):
             ex = exchanges[name]
-            lv, per = ex["lv"], ex["per"]
-            wd = ex["t"] * lv.r
-            f, a = R[ex["field"]], base(ex)
+            lv, per, t = ex["lv"], ex["per"], ex["t"]
+            wd = t * lv.r
+            f, a = R[ex["field"]], start_of(lv)
             lane = iota((lv.rows, 128), 1)
-            for g in range(ex["groups"]):
-                count = min(per, ex["slabs"] - g * per)
-                for j in range(count):
-                    i = a + g * per + j
-                    c = j * wd
-                    below = roll(R[f"zr_{name}"][0, g], -wd - c)
-                    above = roll(R[f"zr_{name}"][1, g], B - c)
-                    v = jnp.where(lane < B + wd, above, jnp.where(lane >= 128 - wd, below, 0.0))
-                    use(i, jnp.where(lane < B, f[i, 8 : 8 + lv.rows, :], v))
+
+            def put(i, below, above):
+                v = jnp.where(lane < B + wd, above, jnp.where(lane >= 128 - wd, below, 0.0))
+                use(i, jnp.where(lane < B, f[i, 8 : 8 + lv.rows, :], v))
+
+            for j in range(lv.n):
+                g, c = j // per, j % per * wd
+                put(a + j, roll(R[f"zr_{name}"][0, g], -wd - c), roll(R[f"zr_{name}"][1, g], B - c))
+            if ex["wide"]:
+                edge = jnp.where(gx == 0, 1 + lv.n, 1)
+                for j in range(t):
+                    c0, c1 = j * wd, (lv.n - t + j - (ex["groups"] - 1) * per) * wd
+                    one = jnp.where(gx == 0, (-wd - c0) % 128, (-wd - c1) % 128)
+                    two = jnp.where(gx == 0, (B - c0) % 128, (B - c1) % 128)
+                    put(edge + j, pltpu.roll(R[f"zx_{name}"][0], one, 1), pltpu.roll(R[f"zx_{name}"][1], two, 1))
 
         def beside_of(lv, ref, a):
             rows = lv.rows
@@ -313,7 +335,7 @@
         def span(lv, far):
             return lv.n + far, 1 + gx * (lv.h - far)
 
-        def relax(lv, src, dst, far, unroll=2):
+        def relax(lv, src, dst, far):
             k = lv.k
             count, a0 = span(lv, far)
 
@@ -325,7 +347,7 @@
                 R[f"{dst}{k}"][a, 8 : 8 + lv.rows, :] = c * KEEP + (e + w * v)
                 return carry
 
-            loop(count, one, 0, unroll)
+            loop(count, one, 0, lv.unroll)
 
         def weigh(lv):
             k = lv.k
@@ -359,7 +381,7 @@
                 t[j] = v
                 return c
 
-            loop(half, one, 0, 2)
+            loop(half, one, 0, lv.unroll // 2)
             wide = iota((half, 128), 1) < B
 
             def two(j, c):
@@ -372,7 +394,7 @@
                     R["l3"][j, 0:half, :] = v
                 return c
 
-            loop(half, two, 0, 2)
+            loop(half, two, 0, 12)
 
         def left_of(lv, src):
             k = lv.k
@@ -401,7 +423,7 @@
                 u[j, pl.ds(shift + 1, m, stride=2), :] = v
                 return c
 
-            loop(half + nxt_far, put, 0, 2)
+            loop(half + nxt_far, put, 0, 7)
 
         def add_up(lv):
             k = lv.k
@@ -419,48 +441,36 @@
                     R[f"b{k}"][a, 8 : 8 + lv.rows, :] = R[f"a{k}"][a, 8 : 8 + lv.rows, :] + p
                 return c
 
-            loop((lv.n + 4) // 2, one, 0, 2)
-
-        def gather_a(name):
-            a = R[f"{name}a"]
-            out = []
-            for d, to in enumerate(others):
-                out.append(pltpu.make_async_remote_copy(
-                    src_ref=a.at[mine], dst_ref=a.at[mine], send_sem=R[f"{name}a_send"].at[d],
-                    recv_sem=R[f"{name}a_recv"].at[d], device_id=to, device_id_type=MESH))
-            return out
-
-        def gather_b(name):
-            b = R[f"{name}b"]
-            out = []
-            for d, to in enumerate(lines):
-                out.append(pltpu.make_async_remote_copy(
-                    src_ref=b.at[:, gz], dst_ref=b.at[:, gz], send_sem=R[f"{name}b_send"].at[d],
-                    recv_sem=R[f"{name}b_recv"].at[d], device_id=to, device_id_type=MESH))
-            return out
+            loop((lv.n + 4) // 2, one, 0, 7)
+
+        def gather_copy(name, dx, dy, dz):
+            g = R[name]
+            here = g.at[:, gz, pl.ds(mine, 1), :]
+            return pltpu.make_async_remote_copy(
+                src_ref=here, dst_ref=here, send_sem=R[f"{name}_send"].at[dz], recv_sem=R[f"{name}_recv"].at[gz],
+                device_id=device(dx, dy, dz), device_id_type=MESH)
 
         def gather_start(name, rows):
             for p, v in enumerate(rows):
-                R[f"{name}a"][mine, p : p + 1, :] = v
-            for copy in gather_a(name):
-                copy.start()
-
-        def gather_middle(name, count):
-            for copy in gather_a(name):
-                copy.wait_recv()
-            for p in range(count):
-                for j in range(plane):
-                    R[f"{name}b"][p, gz, j : j + 1, :] = R[f"{name}a"][j, p : p + 1, :]
-            for copy in gather_b(name):
-                copy.start()
+                R[name][p, gz, pl.ds(mine, 1), :] = v
+            for to in others:
+                gather_copy(name, *to).start()
+
+        def gather_line(name, dz):
+            z = lax.rem(gz + dz, nz)
+            g = R[name]
+            part = g.at[:, z, pl.ds(0, plane - 1), :] if dz == 0 else g.at[:, z]
+            return pltpu.make_async_remote_copy(
+                src_ref=part, dst_ref=part, send_sem=R[f"{name}_send"].at[dz], recv_sem=R[f"{name}_recv"].at[z],
+                device_id=device(1, 0, 0), device_id_type=MESH)
 
         def gather_end(name):
-            for copy in gather_b(name):
-                copy.wait_recv()
+            for dz in range(nz):
+                gather_line(name, dz).wait_recv()
 
         def gather_sent(name):
-            for copy in gather_a(name) + gather_b(name):
-                copy.wait_send()
+            for dz in range(nz):
+                gather_line(name, dz).wait_send()
 
         def local_vector():
             wide = planes * 128
@@ -475,7 +485,7 @@
 
         def by_device(name, dst):
             for p in range(planes):
-                v = R[f"{name}b"][p].reshape(plane * line, 128)
+                v = R[name][p].reshape(plane * line, 128)
                 R[dst][128 * p : 128 * p + 128, :] = v.T
 
         lv0, lv1, lv2 = levels
@@ -494,27 +504,27 @@
         take("sgr", "sg")
         y_pack("sg")
         z_pack("sg")
-        pl.semaphore_wait(barrier, len(others) + len(lines))
-        for axis in "xyz":
-            send("sg", axis)
         inputs[1].wait()
         take("rer", "s0")
-        send("s0", "x")
+        y_pack("s0")
+        z_pack("s0")
+        restrict(lv0, coefficient(lv0), "s")
+        y_pack("s1")
+        z_pack("s1")
+        restrict(lv1, coefficient(lv1), "s")
+        y_pack("s2")
+        z_pack("s2")
+        restrict(lv2, coefficient(lv2), "s")
+        vector3 = local_vector()
         inputs[2].wait()
         take("rsr", "f0")
-        restrict(lv0, coefficient(lv0), "s")
-        send("s1", "x")
-        restrict(lv1, coefficient(lv1), "s")
-        send("s2", "x")
-        restrict(lv2, coefficient(lv2), "s")
-        gather_start("gs", local_vector())
-        arrive("s0", "x")
-        y_pack("s0")
-        send("s0", "y")
-
-        for axis in "xyz":
-            arrive("sg", axis)
-        sent("sg", "x")
+        pl.semaphore_wait(barrier, len(others))
+        send("sg")
+        for k in range(SPLIT):
+            send(f"s{k}")
+        gather_start("gs", vector3)
+        arrive("sg")
+        sent("sg")
         y_unpack("sg")
 
         def keep_guess(i, v):
@@ -530,36 +540,14 @@
             R["f0"][a, 8 : 8 + lv0.rows, :] = jnp.where(R["own"][...] > 0.0, f, 0.0)
             return carry
 
-        loop(B, first_residual, 0, 2)
-        send("f0", "x")
-        for k in (1, 2):
-            arrive(f"s{k}", "x")
-            y_pack(f"s{k}")
-            send(f"s{k}", "y")
-        arrive("s0", "y")
-        sent("s0", "x")
-        y_unpack("s0")
-        z_pack("s0")
-        arrive("f0", "x")
-        y_pack("f0")
-        send("f0", "y")
-        send("s0", "z")
-        gather_middle("gs", planes)
-        arrive("f0", "y")
-        sent("f0", "x")
+        loop(B, first_residual, 0, lv0.unroll)
+        pack_send("f0")
+        for lv in levels:
+            arrive(f"s{lv.k}")
+            y_unpack(f"s{lv.k}")
+            weigh(lv)
+        arrive("f0")
         y_unpack("f0")
-        z_pack("f0")
-        send("f0", "z")
-        for k in (1, 2):
-            arrive(f"s{k}", "y")
-            sent(f"s{k}", "x")
-            y_unpack(f"s{k}")
-            z_pack(f"s{k}")
-            send(f"s{k}", "z")
-        arrive("s0", "z")
-        weigh(lv0)
-        arrive("f0", "z")
-
         begin(lv0)
 
         def first_relax(lv):
@@ -573,33 +561,22 @@
                 R[f"a{k}"][a, 8 : 8 + lv.rows, :] = c * (1.0 + KEEP) + w * v
                 return carry
 
-            loop(count, one, 0, 2)
+            loop(count, one, 0, lv.unroll)
 
         first_relax(lv0)
         restrict(lv0, left_of(lv0, "a"), "f")
 
-        def deeper(lv, fill):
-            k = lv.k
-            name = f"f{k}"
-            send(name, "x")
-            fill()
-            arrive(name, "x")
-            y_pack(name)
-            send(name, "y")
-            arrive(name, "y")
-            sent(name, "x")
+        def deeper(lv):
+            name = f"f{lv.k}"
+            pack_send(name)
+            arrive(name)
             y_unpack(name)
-            z_pack(name)
-            send(name, "z")
-            arrive(f"s{k}", "z")
-            weigh(lv)
-            arrive(name, "z")
             begin(lv)
             first_relax(lv)
             restrict(lv, left_of(lv, "a"), "f")
 
-        deeper(lv1, lambda: None)
-        deeper(lv2, lambda: None)
+        deeper(lv1)
+        deeper(lv2)
         gather_start("gf", local_vector())
 
         gather_end("gs")
@@ -653,7 +630,6 @@
             return out
 
         s4 = coarser(lambda x, y: tile("s3", x, y))
-        gather_middle("gf", planes)
         gather_end("gf")
         by_device("gf", "f3")
         e = {}
@@ -773,11 +749,10 @@
             return upper + R["f0"][a, 8 : 8 + lv0.rows, :] * c, lower + ap * c
 
         zero = jnp.zeros((lv0.rows, 128), F32)
-        upper, lower = loop(B, image, (zero, zero), 2)
+        upper, lower = loop(B, image, (zero, zero), lv0.unroll)
         gather_start("gr", [jnp.sum(v, axis=0, keepdims=True) for v in (upper, lower)])
-        gather_middle("gr", 2)
         gather_end("gr")
-        sums = [total(jnp.sum(R["grb"][p], axis=0)) for p in range(2)]
+        sums = [total(jnp.sum(R["gr"][p], axis=0)) for p in range(2)]
         step_length = sums[0] / sums[1]
 
         def finish(x, c):
@@ -789,10 +764,10 @@
             res_ref[x] = (f - step_length * q)[:, 0:B]
             return c
 
-        loop(B, finish, 0, 2)
+        loop(B, finish, 0, 4)
         for name in exchanges:
-            for axis in "yz":
-                sent(name, axis)
+            if name != "sg":
+                sent(name)
         for name in ("gs", "gf", "gr"):
             gather_sent(name)
 

time: 94.2 us -> 71.1 us (0.75)
  Pallas kernels: 90 us -> 66.8 us
    pallas_call x1, Pallas kernels: 90 us -> 66.8 us  [body(): pl.pallas_call(kernel, out_shape=(out, out), in_specs=[pl.BlockSpec(memor...]
where the time goes in v2:
time: 71.1 us; the launch traced here: 71 us
  Pallas kernels  66.8 us (94%)
  local copies, waits for them, and re-layouts  3.47 us (5%)
    pallas_call x1, Pallas kernels, body(): pl.pallas_call(kernel, out_shape=(out, out), in_specs=[pl.BlockSpec(memor...  66.8 us
    unnamed x4, local copies, waits for them, and re-layouts  3.47 us

profile of v2, /device:TPU:1, one launch (start us, length us, event | category | flops | bytes accessed | tf_op | source)
XLA Modules:
  0.0 71.0 jit_solution(17247387390899970817)
XLA Ops:
  0.6 66.8 %cg_step.1 = (f32[48,48,48]{2,1,0:T(8,128)}, f32[48,48,48]{2,1,0:T(8,128)}) custom-call(f32[48,48,48]{2,1,0:T(8,128)} %rs_ref.1, f32[48,48,48]{2,1,0:T(8,128)} %sg_ref.1, f32[48,48,48]{2,1,0:T(8,128)} %re_ref.1), custom_call_target="tpu_custom_call" | custom-call | tf_op jit(solution)/shard_map/cg_step/pallas_call | solution.py:784
  67.5 0.0 copy-start
  67.5 2.5 %copy.7 = f32[48,48,48]{2,1,0:T(8,128)} copy(f32[48,48,48]{2,1,0:T(8,128)} %get-tuple-element.4) | data formatting | bytes 884736
  69.9 0.0 copy-done
  69.9 1.0 %copy.8 = f32[48,48,48]{2,1,0:T(8,128)} copy(f32[48,48,48]{2,1,0:T(8,128)S(1)} %copy-done) | data formatting | bytes 884736
Async XLA Ops:
  67.5 2.5 %copy-start = (f32[48,48,48]{2,1,0:T(8,128)S(1)}, f32[48,48,48]{2,1,0:T(8,128)}, u32[]{:S(2)}) copy-start(f32[48,48,48]{2,1,0:T(8,128)} %get-tuple-element.5) | copy-start | bytes 1327108

commit v3 on v2

--- a/solution.py
+++ b/solution.py
@@ -76,6 +76,7 @@
     n3 = B >> SPLIT
     groups = n3 * n3
     planes = -(-groups * 8 // 128)
+    packed = -(-groups * n3 // 128)
     q3, q4 = 0.25**3, 0.25**4
     line = nz
     plane = nx * ny
@@ -96,9 +97,8 @@
         if wide:
             scratch[f"yx_{name}"] = pltpu.VMEM((2, t, t, 128), F32)
             scratch[f"zx_{name}"] = pltpu.VMEM((2, lv.rows, 128), F32)
-        count = 17 if wide else 5
-        scratch[f"send_{name}"] = pltpu.SemaphoreType.DMA((count,))
-        scratch[f"recv_{name}"] = pltpu.SemaphoreType.DMA((count,))
+        scratch[f"send_{name}"] = pltpu.SemaphoreType.DMA
+        scratch[f"recv_{name}"] = pltpu.SemaphoreType.DMA
         exchanges[name] = ex
 
     for lv in levels:
@@ -114,10 +114,11 @@
     add_exchange("sg", 0, "sg", 1, False)
     scratch["ap"] = pltpu.VMEM((B, levels[0].rows, 128), F32)
     scratch["own"] = pltpu.VMEM((levels[0].rows, 128), F32)
-    for name, count in (("gs", planes), ("gf", planes), ("gr", 2)):
+    for name, count in (("gs", packed), ("gf", packed), ("gr", 1)):
         scratch[name] = pltpu.VMEM((count, line, plane, 128), F32)
-        scratch[f"{name}_send"] = pltpu.SemaphoreType.DMA((line,))
-        scratch[f"{name}_recv"] = pltpu.SemaphoreType.DMA((line,))
+        scratch[f"{name}_send"] = pltpu.SemaphoreType.DMA
+        scratch[f"{name}_recv"] = pltpu.SemaphoreType.DMA
+    scratch["count"] = pltpu.VMEM((1024, 128), F32)
     scratch["l3"] = pltpu.VMEM((n3, 8, 128), F32)
     for name in ("s3", "f3", "w3", "e3"):
         scratch[name] = pltpu.VMEM((planes * 128, 128), F32)
@@ -182,7 +183,7 @@
                 own = (lane < B) & (row >= lv.h) & (row < lv.h + lv.n)
                 R["own"][...] = jnp.where(own, 1.0, 0.0)
         for name, ex in exchanges.items():
-            for m in ("yr", "zr") + (("yx", "zx") if ex["wide"] else ()):
+            for m in ("yr", "yx", "zr", "zx") if ex["wide"] else ("yr", "zr"):
                 ref = R[f"{m}_{name}"]
                 ref[...] = jnp.zeros(ref.shape, F32)
 
@@ -194,14 +195,17 @@
                     if dx or dy or dz:
                         others.append((dx, dy, dz))
 
+        def hops(to):
+            dx, dy, dz = to
+            return dx + min(dy, ny - dy) + min(dz % 4, 4 - dz % 4) + min(dz // 4, nz // 4 - dz // 4)
+
+        others.sort(key=lambda to: (-hops(to), to))
+
         def device(dx, dy, dz):
             return {"gx": lax.rem(gx + dx, nx), "gy": lax.rem(gy + dy, ny), "gz": lax.rem(gz + dz, nz)}
 
         for to in others:
             pl.semaphore_signal(barrier, inc=1, device_id=device(*to), device_id_type=MESH)
-
-        def exists(at, n, way):
-            return at > 0 if way < 0 else at < n - 1
 
         def messages(name):
             ex = exchanges[name]
@@ -230,29 +234,50 @@
                         out.append((zs.at[i, group, here, :], zx.at[1 - i, there, :], 1, yway, way))
             return out
 
-        def each(name, f, getting):
-            for i, (s, d, ox, oy, oz) in enumerate(messages(name)):
+        def guarded(cond, f):
+            if cond is None:
+                f()
+            else:
+                pl.when(cond)(f)
+
+        def send(name):
+            for src, dst, ox, oy, oz in messages(name):
                 copy = pltpu.make_async_remote_copy(
-                    src_ref=s, dst_ref=d, send_sem=R[f"send_{name}"].at[i], recv_sem=R[f"recv_{name}"].at[i],
-                    device_id={"gx": lax.rem(gx + ox, nx), "gy": gy + oy, "gz": gz + oz}, device_id_type=MESH)
+                    src_ref=src, dst_ref=dst, send_sem=R[f"send_{name}"], recv_sem=R[f"recv_{name}"],
+                    device_id=device(ox, oy % ny, oz % nz), device_id_type=MESH)
                 cond = None
                 for at, n, way in ((gy, ny, oy), (gz, nz, oz)):
                     if way:
-                        there = exists(at, n, -way if getting else way)
+                        there = at > 0 if way < 0 else at < n - 1
                         cond = there if cond is None else cond & there
-                if cond is None:
-                    f(copy)
-                else:
-                    pl.when(cond)(lambda copy=copy: f(copy))
-
-        def send(name):
-            each(name, lambda copy: copy.start(), False)
+                guarded(cond, copy.start)
+
+        def counted(size, send_sem, recv_sem):
+            rows = R["count"].at[pl.ds(0, size), :]
+            return pltpu.make_async_remote_copy(
+                src_ref=rows, dst_ref=rows, send_sem=send_sem, recv_sem=recv_sem,
+                device_id=device(1, 0, 0), device_id_type=MESH)
+
+        def in_all(name, getting):
+            sizes = [(src.shape, oy, oz) for src, _, _, oy, oz in messages(name)]
+            for y, at_y in ((0, gy == 0), (1, (gy > 0) & (gy < ny - 1)), (2, gy == ny - 1)):
+                for z, at_z in ((0, gz == 0), (1, (gz > 0) & (gz < nz - 1)), (2, gz == nz - 1)):
+                    rows = 0
+                    for shape, oy, oz in sizes:
+                        oy, oz = (-oy, -oz) if getting else (oy, oz)
+                        if y + oy in (0, 1, 2) and z + oz in (0, 1, 2):
+                            count = 1
+                            for d in shape[:-1]:
+                                count *= d
+                            rows += count
+                    copy = counted(rows, R[f"send_{name}"], R[f"recv_{name}"])
+                    pl.when(at_y & at_z)(copy.wait_recv if getting else copy.wait_send)
 
         def arrive(name):
-            each(name, lambda copy: copy.wait_recv(), True)
+            in_all(name, True)
 
         def sent(name):
-            each(name, lambda copy: copy.wait_send(), False)
+            in_all(name, False)
 
         def y_pack(name):
             ex = exchanges[name]
@@ -270,9 +295,10 @@
             f, a = R[ex["field"]], start_of(lv)
             keep = iota((t, 128), 1) < B
             edge = jnp.where(gx == 0, 1 + lv.n, 1)
-            for side, row in ((0, lv.first - t), (1, lv.first + lv.n)):
+            for side, row, ok in ((0, lv.first - t, gy > 0), (1, lv.first + lv.n, gy < ny - 1)):
                 for i in range(m):
                     v = R[f"yr_{name}"][side, i]
+                    v = v if ex["wide"] else jnp.where(ok, v, 0.0)
                     f[a + i, row : row + t, :] = jnp.where(keep, v, 0.0)
                     f[a + i + m, row : row + t, :] = jnp.where(keep, roll(v, 64), 0.0)
                 if ex["wide"]:
@@ -311,6 +337,8 @@
             lane = iota((lv.rows, 128), 1)
 
             def put(i, below, above):
+                if not ex["wide"]:
+                    below, above = jnp.where(gz > 0, below, 0.0), jnp.where(gz < nz - 1, above, 0.0)
                 v = jnp.where(lane < B + wd, above, jnp.where(lane >= 128 - wd, below, 0.0))
                 use(i, jnp.where(lane < B, f[i, 8 : 8 + lv.rows, :], v))
 
@@ -447,7 +475,7 @@
             g = R[name]
             here = g.at[:, gz, pl.ds(mine, 1), :]
             return pltpu.make_async_remote_copy(
-                src_ref=here, dst_ref=here, send_sem=R[f"{name}_send"].at[dz], recv_sem=R[f"{name}_recv"].at[gz],
+                src_ref=here, dst_ref=here, send_sem=R[f"{name}_send"], recv_sem=R[f"{name}_recv"],
                 device_id=device(dx, dy, dz), device_id_type=MESH)
 
         def gather_start(name, rows):
@@ -456,35 +484,29 @@
             for to in others:
                 gather_copy(name, *to).start()
 
-        def gather_line(name, dz):
-            z = lax.rem(gz + dz, nz)
-            g = R[name]
-            part = g.at[:, z, pl.ds(0, plane - 1), :] if dz == 0 else g.at[:, z]
-            return pltpu.make_async_remote_copy(
-                src_ref=part, dst_ref=part, send_sem=R[f"{name}_send"].at[dz], recv_sem=R[f"{name}_recv"].at[z],
-                device_id=device(1, 0, 0), device_id_type=MESH)
+        def gathered(name):
+            size = len(others) * R[name].shape[0]
+            return counted(size, R[f"{name}_send"], R[f"{name}_recv"])
 
         def gather_end(name):
-            for dz in range(nz):
-                gather_line(name, dz).wait_recv()
+            gathered(name).wait_recv()
 
         def gather_sent(name):
-            for dz in range(nz):
-                gather_line(name, dz).wait_send()
+            gathered(name).wait_send()
 
         def local_vector():
-            wide = planes * 128
+            wide = packed * 128
             v = R["l3"][...].reshape(n3 * 8, 128)
             l, c = iota((128, wide), 0), iota((128, wide), 1)
-            table = jnp.where((l == (c & 7) * (1 << SPLIT)) & ((c & 7) < n3) & (c < groups * 8), 1.0, 0.0).astype(BF16)
+            table = jnp.where((l == c % n3 * (1 << SPLIT)) & (c < groups * n3), 1.0, 0.0).astype(BF16)
             v = picked(v, table)
             row, c = iota((n3 * 8, wide), 0), iota((n3 * 8, wide), 1)
-            keep = ((row & 7) < n3) & ((c >> 3) == (row >> 3) * n3 + (row & 7))
+            keep = ((row & 7) < n3) & (c // n3 == (row >> 3) * n3 + (row & 7))
             v = jnp.sum(jnp.where(keep, v, 0.0), axis=0, keepdims=True)
-            return [v[:, 128 * p : 128 * p + 128] for p in range(planes)]
+            return [v[:, 128 * p : 128 * p + 128] for p in range(packed)]
 
         def by_device(name, dst):
-            for p in range(planes):
+            for p in range(packed):
                 v = R[name][p].reshape(plane * line, 128)
                 R[dst][128 * p : 128 * p + 128, :] = v.T
 
@@ -614,8 +636,8 @@
         live = row8 < n3
 
         def tile(name, x, y):
-            g = x * n3 + y
-            return R[name][8 * g : 8 * g + 8, :]
+            g = (x * n3 + y) * (n3 if name in ("s3", "f3") else 8)
+            return R[name][g : g + 8, :]
 
         for x, y in cells:
             R["w3"][8 * (x * n3 + y) : 8 * (x * n3 + y) + 8, :] = jnp.where(
@@ -750,9 +772,13 @@
 
         zero = jnp.zeros((lv0.rows, 128), F32)
         upper, lower = loop(B, image, (zero, zero), lv0.unroll)
-        gather_start("gr", [jnp.sum(v, axis=0, keepdims=True) for v in (upper, lower)])
+        upper, lower = (jnp.sum(v, axis=0, keepdims=True) for v in (upper, lower))
+        half = iota((1, 128), 1) < 64
+        gather_start("gr", [jnp.where(half, upper, roll(lower, 64))])
         gather_end("gr")
-        sums = [total(jnp.sum(R["gr"][p], axis=0)) for p in range(2)]
+        v = jnp.sum(R["gr"][0], axis=0)
+        half = iota((8, 128), 1) < 64
+        sums = [total(jnp.where(half, v, 0.0)), total(jnp.where(half, 0.0, v))]
         step_length = sums[0] / sums[1]
 
         def finish(x, c):

time: 71.1 us -> 66.9 us (0.941)
  Pallas kernels: 66.8 us -> 62.7 us
    pallas_call x1, Pallas kernels: 66.8 us -> 62.7 us  [body(): pl.pallas_call(kernel, out_shape=(out, out), in_specs=[pl.BlockSpec(memor...]
where the time goes in v3:
time: 66.9 us; the launch traced here: 66.8 us
  Pallas kernels  62.7 us (94%)
  local copies, waits for them, and re-layouts  3.47 us (5%)
    pallas_call x1, Pallas kernels, body(): pl.pallas_call(kernel, out_shape=(out, out), in_specs=[pl.BlockSpec(memor...  62.7 us
    unnamed x4, local copies, waits for them, and re-layouts  3.47 us

profile of v3, /device:TPU:1, one launch (start us, length us, event | category | flops | bytes accessed | tf_op | source)
XLA Modules:
  0.0 66.8 jit_solution(885593592937255768)
XLA Ops:
  0.6 62.7 %cg_step.1 = (f32[48,48,48]{2,1,0:T(8,128)}, f32[48,48,48]{2,1,0:T(8,128)}) custom-call(f32[48,48,48]{2,1,0:T(8,128)} %rs_ref.1, f32[48,48,48]{2,1,0:T(8,128)} %sg_ref.1, f32[48,48,48]{2,1,0:T(8,128)} %re_ref.1), custom_call_target="tpu_custom_call" | custom-call | tf_op jit(solution)/shard_map/cg_step/pallas_call | solution.py:810
  63.3 0.0 copy-start
  63.3 2.5 %copy.7 = f32[48,48,48]{2,1,0:T(8,128)} copy(f32[48,48,48]{2,1,0:T(8,128)} %get-tuple-element.4) | data formatting | bytes 884736
  65.8 0.0 copy-done
  65.8 1.0 %copy.8 = f32[48,48,48]{2,1,0:T(8,128)} copy(f32[48,48,48]{2,1,0:T(8,128)S(1)} %copy-done) | data formatting | bytes 884736
Async XLA Ops:
  63.3 2.5 %copy-start = (f32[48,48,48]{2,1,0:T(8,128)S(1)}, f32[48,48,48]{2,1,0:T(8,128)}, u32[]{:S(2)}) copy-start(f32[48,48,48]{2,1,0:T(8,128)} %get-tuple-element.5) | copy-start | bytes 1327108

commit v4 on v3

--- a/solution.py
+++ b/solution.py
@@ -119,6 +119,8 @@
         scratch[f"{name}_send"] = pltpu.SemaphoreType.DMA
         scratch[f"{name}_recv"] = pltpu.SemaphoreType.DMA
     scratch["count"] = pltpu.VMEM((1024, 128), F32)
+    for name in ("k2", "k3", "k4", "k5"):
+        scratch[name] = pltpu.SemaphoreType.REGULAR
     scratch["l3"] = pltpu.VMEM((n3, 8, 128), F32)
     for name in ("s3", "f3", "w3", "e3"):
         scratch[name] = pltpu.VMEM((planes * 128, 128), F32)
@@ -144,21 +146,6 @@
 
         for lv in levels:
             k = lv.k
-            z8 = jnp.zeros((8, 128), F32)
-            zs = jnp.zeros((lv.rows, 128), F32)
-            fields = ["e", "a", "b"] + (["sg"] if k == 0 else [])
-            fields = [R[f if f == "sg" else f"{f}{k}"] for f in fields]
-
-            def guard(a, c, fields=fields, lv=lv, z8=z8):
-                for ref in fields:
-                    ref[a, 0:8, :] = z8
-                    ref[a, 8 + lv.rows : 16 + lv.rows, :] = z8
-                return c
-
-            loop(lv.shape[0], guard, 0, 2)
-            for ref in fields:
-                ref[0, 8 : 8 + lv.rows, :] = zs
-                ref[lv.slabs + 1, 8 : 8 + lv.rows, :] = zs
 
             def blank(a, c, k=k, lv=lv):
                 for name in ("f", "s"):
@@ -173,6 +160,66 @@
                 return c
 
             loop(lv.shape[0], blank, 0, 2)
+
+        for name, ex in exchanges.items():
+            for m in ("yr", "yx", "zr", "zx") if ex["wide"] else ("yr", "zr"):
+                ref = R[f"{m}_{name}"]
+                ref[...] = jnp.zeros(ref.shape, F32)
+
+        barrier = pltpu.get_barrier_semaphore()
+        others = []
+        for dz in range(nz):
+            for dx in range(nx):
+                for dy in range(ny):
+                    if dx or dy or dz:
+                        others.append((dx, dy, dz))
+
+        def hops(to):
+            dx, dy, dz = to
+            return dx + min(dy, ny - dy) + min(dz % 4, 4 - dz % 4) + min(dz // 4, nz // 4 - dz // 4)
+
+        others.sort(key=lambda to: (-hops(to), to))
+
+        def device(dx, dy, dz):
+            return {"gx": lax.rem(gx + dx, nx), "gy": lax.rem(gy + dy, ny), "gz": lax.rem(gz + dz, nz)}
+
+        faces = [(1, 0, 0), (0, 1, 0), (0, ny - 1, 0), (0, 0, 1), (0, 0, nz - 1)]
+        two = nz // 8
+        waves = {
+            "k2": faces,
+            "k3": faces[:3] + [(0, 0, two), (0, 0, nz - two)],
+            "k4": [(0, 0, 2 * two), (0, 0, nz - 2 * two)],
+            "k5": [to for to in others if to[2] == 0],
+        }
+
+        def greet(name):
+            for to in waves[name]:
+                pl.semaphore_signal(R[name], inc=1, device_id=device(*to), device_id_type=MESH)
+
+        def greeted(name):
+            pl.semaphore_wait(R[name], len(waves[name]))
+
+        for to in faces:
+            pl.semaphore_signal(barrier, inc=1, device_id=device(*to), device_id_type=MESH)
+
+        for lv in levels:
+            k = lv.k
+            z8 = jnp.zeros((8, 128), F32)
+            zs = jnp.zeros((lv.rows, 128), F32)
+            fields = ["e", "a", "b"] + (["sg"] if k == 0 else [])
+            fields = [R[f if f == "sg" else f"{f}{k}"] for f in fields]
+
+            def guard(a, c, fields=fields, lv=lv, z8=z8):
+                for ref in fields:
+                    ref[a, 0:8, :] = z8
+                    ref[a, 8 + lv.rows : 16 + lv.rows, :] = z8
+                return c
+
+            loop(lv.shape[0], guard, 0, 2)
+            for ref in fields:
+                ref[0, 8 : 8 + lv.rows, :] = zs
+                ref[lv.slabs + 1, 8 : 8 + lv.rows, :] = zs
+
             lane, row = iota((lv.rows, 128), 1), iota((lv.rows, 128), 0)
             wd = lv.h * lv.r
             ok = (lane < B) | ((lane < B + wd) & (gz < nz - 1)) | ((lane >= 128 - wd) & (gz > 0))
@@ -182,30 +229,6 @@
             if k == 0:
                 own = (lane < B) & (row >= lv.h) & (row < lv.h + lv.n)
                 R["own"][...] = jnp.where(own, 1.0, 0.0)
-        for name, ex in exchanges.items():
-            for m in ("yr", "yx", "zr", "zx") if ex["wide"] else ("yr", "zr"):
-                ref = R[f"{m}_{name}"]
-                ref[...] = jnp.zeros(ref.shape, F32)
-
-        barrier = pltpu.get_barrier_semaphore()
-        others = []
-        for dz in range(nz):
-            for dx in range(nx):
-                for dy in range(ny):
-                    if dx or dy or dz:
-                        others.append((dx, dy, dz))
-
-        def hops(to):
-            dx, dy, dz = to
-            return dx + min(dy, ny - dy) + min(dz % 4, 4 - dz % 4) + min(dz // 4, nz // 4 - dz // 4)
-
-        others.sort(key=lambda to: (-hops(to), to))
-
-        def device(dx, dy, dz):
-            return {"gx": lax.rem(gx + dx, nx), "gy": lax.rem(gy + dy, ny), "gz": lax.rem(gz + dz, nz)}
-
-        for to in others:
-            pl.semaphore_signal(barrier, inc=1, device_id=device(*to), device_id_type=MESH)
 
         def messages(name):
             ex = exchanges[name]
@@ -530,21 +553,25 @@
         take("rer", "s0")
         y_pack("s0")
         z_pack("s0")
+        pl.semaphore_wait(barrier, len(faces))
+        send("sg")
+        greet("k2")
+        inputs[2].wait()
+        take("rsr", "f0")
         restrict(lv0, coefficient(lv0), "s")
+        greeted("k2")
+        greet("k3")
         y_pack("s1")
         z_pack("s1")
         restrict(lv1, coefficient(lv1), "s")
         y_pack("s2")
         z_pack("s2")
+        greeted("k3")
+        greet("k4")
+        for k in range(SPLIT):
+            send(f"s{k}")
         restrict(lv2, coefficient(lv2), "s")
         vector3 = local_vector()
-        inputs[2].wait()
-        take("rsr", "f0")
-        pl.semaphore_wait(barrier, len(others))
-        send("sg")
-        for k in range(SPLIT):
-            send(f"s{k}")
-        gather_start("gs", vector3)
         arrive("sg")
         sent("sg")
         y_unpack("sg")
@@ -563,7 +590,11 @@
             return carry
 
         loop(B, first_residual, 0, lv0.unroll)
+        greeted("k4")
+        greet("k5")
         pack_send("f0")
+        greeted("k5")
+        gather_start("gs", vector3)
         for lv in levels:
             arrive(f"s{lv.k}")
             y_unpack(f"s{lv.k}")
@@ -814,7 +845,7 @@
                 out_specs=(pl.BlockSpec(memory_space=pltpu.VMEM),) * 2,
                 scratch_shapes=scratch,
                 compiler_params=pltpu.CompilerParams(
-                    collective_id=0, has_side_effects=True, vmem_limit_bytes=60 * 2**20
+                    collective_id=0, has_side_effects=True, vmem_limit_bytes=51 * 2**20
                 ),
                 name="cg_step",
             )(right_side, start_guess, reaction)

time: 66.9 us -> 62.4 us (0.933)
  Pallas kernels: 62.7 us -> 59.6 us
  local copies, waits for them, and re-layouts: 3.47 us -> 2.03 us
    pallas_call x1, Pallas kernels: 62.7 us -> 59.6 us  [body(): pl.pallas_call(kernel, out_shape=(out, out), in_specs=[pl.BlockSpec(memor...]
    unnamed x4 -> x2, local copies, waits for them, and re-layouts: 3.47 us -> 2.03 us
where the time goes in v4:
time: 62.4 us; the launch traced here: 62.3 us
  Pallas kernels  59.6 us (96%)
  local copies, waits for them, and re-layouts  2.03 us (3%)
  between operations  0.64 us (1%)
    pallas_call x1, Pallas kernels, body(): pl.pallas_call(kernel, out_shape=(out, out), in_specs=[pl.BlockSpec(memor...  59.6 us
    unnamed x2, local copies, waits for them, and re-layouts  2.03 us

profile of v4, /device:TPU:1, one launch (start us, length us, event | category | flops | bytes accessed | tf_op | source)
XLA Modules:
  0.0 62.3 jit_solution(940502435337163837)
XLA Ops:
  0.6 59.6 %cg_step.1 = (f32[48,48,48]{2,1,0:T(8,128)S(1)}, f32[48,48,48]{2,1,0:T(8,128)S(1)}) custom-call(f32[48,48,48]{2,1,0:T(8,128)} %rs_ref.1, f32[48,48,48]{2,1,0:T(8,128)} %sg_ref.1, f32[48,48,48]{2,1,0:T(8,128)} %re_ref.1), custom_call_target="tpu_custom_call" | custom-call | tf_op jit(solution)/shard_map/cg_step/pallas_call | solution.py:841
  60.3 1.0 %copy.7 = f32[48,48,48]{2,1,0:T(8,128)} copy(f32[48,48,48]{2,1,0:T(8,128)S(1)} %get-tuple-element.4) | data formatting | bytes 884736
  61.3 1.0 %copy.8 = f32[48,48,48]{2,1,0:T(8,128)} copy(f32[48,48,48]{2,1,0:T(8,128)S(1)} %get-tuple-element.5) | data formatting | bytes 884736

commit v5 on v4

--- a/solution.py
+++ b/solution.py
@@ -65,7 +65,7 @@
         self.rows = 8 * self.tiles
         self.slabs = self.n + self.h
         self.first = 8 + self.h
-        self.unroll = 14 if k == 0 else 28
+        self.unroll = 26 if k == 0 else 28
         self.shape = (self.slabs + 2, self.rows + 16, 128)
 
 
@@ -263,8 +263,10 @@
             else:
                 pl.when(cond)(f)
 
-        def send(name):
-            for src, dst, ox, oy, oz in messages(name):
+        def send(name, only=None):
+            batch = [m for m in messages(name) if only is None or only(*m[2:])]
+            batch.sort(key=lambda m: -(m[2] + abs(m[3]) + 2 * abs(m[4])))
+            for src, dst, ox, oy, oz in batch:
                 copy = pltpu.make_async_remote_copy(
                     src_ref=src, dst_ref=dst, send_sem=R[f"send_{name}"], recv_sem=R[f"recv_{name}"],
                     device_id=device(ox, oy % ny, oz % nz), device_id_type=MESH)
@@ -348,9 +350,11 @@
                 R[f"zs_{name}"][1, g] = high
 
         def pack_send(name):
+            send(name, lambda ox, oy, oz: not oy and not oz)
+            z_pack(name)
+            send(name, lambda ox, oy, oz: oz)
             y_pack(name)
-            z_pack(name)
-            send(name)
+            send(name, lambda ox, oy, oz: oy and not oz)
 
         def z_unpacked(name, use):
             ex = exchanges[name]
@@ -568,8 +572,7 @@
         z_pack("s2")
         greeted("k3")
         greet("k4")
-        for k in range(SPLIT):
-            send(f"s{k}")
+        send("s0")
         restrict(lv2, coefficient(lv2), "s")
         vector3 = local_vector()
         arrive("sg")
@@ -593,12 +596,15 @@
         greeted("k4")
         greet("k5")
         pack_send("f0")
-        greeted("k5")
-        gather_start("gs", vector3)
-        for lv in levels:
+        send("s1")
+        send("s2")
+
+        def weigh_at(lv):
             arrive(f"s{lv.k}")
             y_unpack(f"s{lv.k}")
             weigh(lv)
+
+        weigh_at(lv0)
         arrive("f0")
         y_unpack("f0")
         begin(lv0)
@@ -619,17 +625,20 @@
         first_relax(lv0)
         restrict(lv0, left_of(lv0, "a"), "f")
 
-        def deeper(lv):
+        def deeper(lv, fill):
             name = f"f{lv.k}"
             pack_send(name)
+            fill()
+            weigh_at(lv)
             arrive(name)
             y_unpack(name)
             begin(lv)
             first_relax(lv)
             restrict(lv, left_of(lv, "a"), "f")
 
-        deeper(lv1)
-        deeper(lv2)
+        greeted("k5")
+        deeper(lv1, lambda: None)
+        deeper(lv2, lambda: gather_start("gs", vector3))
         gather_start("gf", local_vector())
 
         gather_end("gs")

time: 62.4 us -> 60.4 us (0.968)
  Pallas kernels: 59.6 us -> 57.6 us
    pallas_call x1, Pallas kernels: 59.6 us -> 57.6 us  [body(): pl.pallas_call(kernel, out_shape=(out, out), in_specs=[pl.BlockSpec(memor...]
where the time goes in v5:
time: 60.4 us; the launch traced here: 60.3 us
  Pallas kernels  57.6 us (95%)
  local copies, waits for them, and re-layouts  2.03 us (3%)
  between operations  0.64 us (1%)
    pallas_call x1, Pallas kernels, body(): pl.pallas_call(kernel, out_shape=(out, out), in_specs=[pl.BlockSpec(memor...  57.6 us
    unnamed x2, local copies, waits for them, and re-layouts  2.03 us

profile of v5, /device:TPU:1, one launch (start us, length us, event | category | flops | bytes accessed | tf_op | source)
XLA Modules:
  0.0 60.3 jit_solution(14854784050437080843)
XLA Ops:
  0.6 57.6 %cg_step.1 = (f32[48,48,48]{2,1,0:T(8,128)S(1)}, f32[48,48,48]{2,1,0:T(8,128)S(1)}) custom-call(f32[48,48,48]{2,1,0:T(8,128)} %rs_ref.1, f32[48,48,48]{2,1,0:T(8,128)} %sg_ref.1, f32[48,48,48]{2,1,0:T(8,128)} %re_ref.1), custom_call_target="tpu_custom_call" | custom-call | tf_op jit(solution)/shard_map/cg_step/pallas_call | solution.py:850
  58.3 1.0 %copy.7 = f32[48,48,48]{2,1,0:T(8,128)} copy(f32[48,48,48]{2,1,0:T(8,128)S(1)} %get-tuple-element.4) | data formatting | bytes 884736
  59.3 1.0 %copy.8 = f32[48,48,48]{2,1,0:T(8,128)} copy(f32[48,48,48]{2,1,0:T(8,128)S(1)} %get-tuple-element.5) | data formatting | bytes 884736

commit v6 on v5

--- a/solution.py
+++ b/solution.py
@@ -65,7 +65,7 @@
         self.rows = 8 * self.tiles
         self.slabs = self.n + self.h
         self.first = 8 + self.h
-        self.unroll = 26 if k == 0 else 28
+        self.unroll = 52 if k == 0 else 28
         self.shape = (self.slabs + 2, self.rows + 16, 128)
 
 
@@ -560,6 +560,7 @@
         pl.semaphore_wait(barrier, len(faces))
         send("sg")
         greet("k2")
+        send("s0", lambda *to: sum(map(abs, to)) == 1)
         inputs[2].wait()
         take("rsr", "f0")
         restrict(lv0, coefficient(lv0), "s")
@@ -572,7 +573,7 @@
         z_pack("s2")
         greeted("k3")
         greet("k4")
-        send("s0")
+        send("s0", lambda *to: sum(map(abs, to)) > 1)
         restrict(lv2, coefficient(lv2), "s")
         vector3 = local_vector()
         arrive("sg")
@@ -830,7 +831,7 @@
             res_ref[x] = (f - step_length * q)[:, 0:B]
             return c
 
-        loop(B, finish, 0, 4)
+        loop(B, finish, 0, 12)
         for name in exchanges:
             if name != "sg":
                 sent(name)

time: 60.4 us -> 59.7 us (0.988)
  Pallas kernels: 57.6 us -> 56.9 us
    pallas_call x1, Pallas kernels: 57.6 us -> 56.9 us  [body(): pl.pallas_call(kernel, out_shape=(out, out), in_specs=[pl.BlockSpec(memor...]
where the time goes in v6:
time: 59.7 us; the launch traced here: 59.6 us
  Pallas kernels  56.9 us (95%)
  local copies, waits for them, and re-layouts  2.03 us (3%)
  between operations  0.64 us (1%)
    pallas_call x1, Pallas kernels, body(): pl.pallas_call(kernel, out_shape=(out, out), in_specs=[pl.BlockSpec(memor...  56.9 us
    unnamed x2, local copies, waits for them, and re-layouts  2.03 us

profile of v6, /device:TPU:1, one launch (start us, length us, event | category | flops | bytes accessed | tf_op | source)
XLA Modules:
  0.0 59.6 jit_solution(172911100597083537)
XLA Ops:
  0.6 56.9 %cg_step.1 = (f32[48,48,48]{2,1,0:T(8,128)S(1)}, f32[48,48,48]{2,1,0:T(8,128)S(1)}) custom-call(f32[48,48,48]{2,1,0:T(8,128)} %rs_ref.1, f32[48,48,48]{2,1,0:T(8,128)} %sg_ref.1, f32[48,48,48]{2,1,0:T(8,128)} %re_ref.1), custom_call_target="tpu_custom_call" | custom-call | tf_op jit(solution)/shard_map/cg_step/pallas_call | solution.py:851
  57.6 1.0 %copy.7 = f32[48,48,48]{2,1,0:T(8,128)} copy(f32[48,48,48]{2,1,0:T(8,128)S(1)} %get-tuple-element.4) | data formatting | bytes 884736
  58.6 1.0 %copy.8 = f32[48,48,48]{2,1,0:T(8,128)} copy(f32[48,48,48]{2,1,0:T(8,128)S(1)} %get-tuple-element.5) | data formatting | bytes 884736

commit v7 on v6

--- a/solution.py
+++ b/solution.py
@@ -92,10 +92,10 @@
         per = 128 // (t * lv.r)
         ex = dict(lv=lv, field=field, t=t, wide=wide, per=per, pairs=lv.n // 2, groups=-(-lv.n // per))
         for d in ("s", "r"):
-            scratch[f"y{d}_{name}"] = pltpu.VMEM((2, ex["pairs"], t, 128), F32)
+            scratch[f"y{d}_{name}"] = pltpu.VMEM((3, ex["pairs"], t, 128), F32)
             scratch[f"z{d}_{name}"] = pltpu.VMEM((2, ex["groups"], lv.rows, 128), F32)
         if wide:
-            scratch[f"yx_{name}"] = pltpu.VMEM((2, t, t, 128), F32)
+            scratch[f"yx_{name}"] = pltpu.VMEM((3, t, t, 128), F32)
             scratch[f"zx_{name}"] = pltpu.VMEM((2, lv.rows, 128), F32)
         scratch[f"send_{name}"] = pltpu.SemaphoreType.DMA
         scratch[f"recv_{name}"] = pltpu.SemaphoreType.DMA
@@ -115,7 +115,7 @@
     scratch["ap"] = pltpu.VMEM((B, levels[0].rows, 128), F32)
     scratch["own"] = pltpu.VMEM((levels[0].rows, 128), F32)
     for name, count in (("gs", packed), ("gf", packed), ("gr", 1)):
-        scratch[name] = pltpu.VMEM((count, line, plane, 128), F32)
+        scratch[name] = pltpu.VMEM((count, line + 1, plane, 128), F32)
         scratch[f"{name}_send"] = pltpu.SemaphoreType.DMA
         scratch[f"{name}_recv"] = pltpu.SemaphoreType.DMA
     scratch["count"] = pltpu.VMEM((1024, 128), F32)
@@ -124,7 +124,7 @@
     scratch["l3"] = pltpu.VMEM((n3, 8, 128), F32)
     for name in ("s3", "f3", "w3", "e3"):
         scratch[name] = pltpu.VMEM((planes * 128, 128), F32)
-    scratch["x3"] = pltpu.VMEM((planes, plane * line, 128), F32)
+    scratch["x3"] = pltpu.VMEM((planes, plane * line + 8, 128), F32)
     scratch["lhs"] = pltpu.VMEM((3, (n3 + 2) * 16, planes * 128), F32)
 
     names = list(scratch)
@@ -534,7 +534,7 @@
 
         def by_device(name, dst):
             for p in range(packed):
-                v = R[name][p].reshape(plane * line, 128)
+                v = R[name][p, 0:line].reshape(plane * line, 128)
                 R[dst][128 * p : 128 * p + 128, :] = v.T
 
         lv0, lv1, lv2 = levels
@@ -746,7 +746,7 @@
             R["e3"][8 * g : 8 * g + 8, :] = e[x, y]
         R["e3"][groups * 8 :, :] = jnp.zeros((planes * 128 - groups * 8, 128), F32)
         for p in range(planes):
-            R["x3"][p] = R["e3"][128 * p : 128 * p + 128, :].T
+            R["x3"][p, 0:128, :] = R["e3"][128 * p : 128 * p + 128, :].T
 
         wide = planes * 128
         slabs3 = n3 + 2
@@ -817,7 +817,7 @@
         half = iota((1, 128), 1) < 64
         gather_start("gr", [jnp.where(half, upper, roll(lower, 64))])
         gather_end("gr")
-        v = jnp.sum(R["gr"][0], axis=0)
+        v = jnp.sum(R["gr"][0, 0:line], axis=0)
         half = iota((8, 128), 1) < 64
         sums = [total(jnp.where(half, v, 0.0)), total(jnp.where(half, 0.0, v))]
         step_length = sums[0] / sums[1]

time: 59.7 us -> 59.7 us (level)
  no operation moved by 1% of the time
where the time goes in v7:
time: 59.7 us; the launch traced here: 59.6 us
  Pallas kernels  57 us (95%)
  local copies, waits for them, and re-layouts  2.03 us (3%)
  between operations  0.64 us (1%)
    pallas_call x1, Pallas kernels, body(): pl.pallas_call(kernel, out_shape=(out, out), in_specs=[pl.BlockSpec(memor...  57 us
    unnamed x2, local copies, waits for them, and re-layouts  2.03 us

profile of v7, /device:TPU:1, one launch (start us, length us, event | category | flops | bytes accessed | tf_op | source)
XLA Modules:
  0.0 59.6 jit_solution(17771948517911542931)
XLA Ops:
  0.6 57.0 %cg_step.1 = (f32[48,48,48]{2,1,0:T(8,128)S(1)}, f32[48,48,48]{2,1,0:T(8,128)S(1)}) custom-call(f32[48,48,48]{2,1,0:T(8,128)} %rs_ref.1, f32[48,48,48]{2,1,0:T(8,128)} %sg_ref.1, f32[48,48,48]{2,1,0:T(8,128)} %re_ref.1), custom_call_target="tpu_custom_call" | custom-call | tf_op jit(solution)/shard_map/cg_step/pallas_call | solution.py:851
  57.6 1.0 %copy.7 = f32[48,48,48]{2,1,0:T(8,128)} copy(f32[48,48,48]{2,1,0:T(8,128)S(1)} %get-tuple-element.4) | data formatting | bytes 884736
  58.6 1.0 %copy.8 = f32[48,48,48]{2,1,0:T(8,128)} copy(f32[48,48,48]{2,1,0:T(8,128)S(1)} %get-tuple-element.5) | data formatting | bytes 884736

commit v8 on v7

--- a/solution.py
+++ b/solution.py
@@ -449,7 +449,7 @@
                     R["l3"][j, 0:half, :] = v
                 return c
 
-            loop(half, two, 0, 12)
+            loop(half, two, 0, 24)
 
         def left_of(lv, src):
             k = lv.k
@@ -478,7 +478,7 @@
                 u[j, pl.ds(shift + 1, m, stride=2), :] = v
                 return c
 
-            loop(half + nxt_far, put, 0, 7)
+            loop(half + nxt_far, put, 0, 13)
 
         def add_up(lv):
             k = lv.k
@@ -496,7 +496,7 @@
                     R[f"b{k}"][a, 8 : 8 + lv.rows, :] = R[f"a{k}"][a, 8 : 8 + lv.rows, :] + p
                 return c
 
-            loop((lv.n + 4) // 2, one, 0, 7)
+            loop((lv.n + 4) // 2, one, 0, 14)
 
         def gather_copy(name, dx, dy, dz):
             g = R[name]
@@ -831,7 +831,7 @@
             res_ref[x] = (f - step_length * q)[:, 0:B]
             return c
 
-        loop(B, finish, 0, 12)
+        loop(B, finish, 0, 24)
         for name in exchanges:
             if name != "sg":
                 sent(name)

time: 59.7 us -> 59.5 us (level)
  no operation moved by 1% of the time
where the time goes in v8:
time: 59.5 us; the launch traced here: 59.4 us
  Pallas kernels  56.7 us (95%)
  local copies, waits for them, and re-layouts  2.03 us (3%)
  between operations  0.64 us (1%)
    pallas_call x1, Pallas kernels, body(): pl.pallas_call(kernel, out_shape=(out, out), in_specs=[pl.BlockSpec(memor...  56.7 us
    unnamed x2, local copies, waits for them, and re-layouts  2.03 us

profile of v8, /device:TPU:1, one launch (start us, length us, event | category | flops | bytes accessed | tf_op | source)
XLA Modules:
  0.0 59.4 jit_solution(9965331359019340169)
XLA Ops:
  0.6 56.7 %cg_step.1 = (f32[48,48,48]{2,1,0:T(8,128)S(1)}, f32[48,48,48]{2,1,0:T(8,128)S(1)}) custom-call(f32[48,48,48]{2,1,0:T(8,128)} %rs_ref.1, f32[48,48,48]{2,1,0:T(8,128)} %sg_ref.1, f32[48,48,48]{2,1,0:T(8,128)} %re_ref.1), custom_call_target="tpu_custom_call" | custom-call | tf_op jit(solution)/shard_map/cg_step/pallas_call | solution.py:851
  57.4 1.0 %copy.7 = f32[48,48,48]{2,1,0:T(8,128)} copy(f32[48,48,48]{2,1,0:T(8,128)S(1)} %get-tuple-element.4) | data formatting | bytes 884736
  58.4 1.0 %copy.8 = f32[48,48,48]{2,1,0:T(8,128)} copy(f32[48,48,48]{2,1,0:T(8,128)S(1)} %get-tuple-element.5) | data formatting | bytes 884736
